TPU v7x, 32 devices: a whole 2x2x4 slice. The times are simulated.
32 devices in a mesh: mp: 4 (over x, core), batch: 8 (over z, y).
Axes of the slice: x: 2, y: 2, z: 4, core: 2. Of those that a mesh axis runs over, the one named last changes fastest.
Arguments:
- tokens: bfloat16 [16384, 768], P(('batch', 'mp')), may hold values from -6 to 6
- seg_ids: int32 [16384], P('batch'), may hold values from 0 to 17, as said below
- counts: int32 [8], P('batch'), may hold values from 128 to 2048, as said below
- gain_attn: float32 [768], replicated, may hold values from 0.5 to 1.5
- gain_ffn: float32 [768], replicated, may hold values from 0.5 to 1.5
- w_qkv: bfloat16 [768, 3, 768], P('batch', None, 'mp'), may hold values from -0.21875 to 0.21875
- dconv_kernel: float32 [3, 3, 768], P(None, None, 'mp'), may hold values from -3 to 3
- w_out: bfloat16 [768, 768], P('mp', 'batch'), may hold values from -1.75 to 1.75
- w_up: bfloat16 [768, 3072], P('batch', 'mp'), may hold values from -0.21875 to 0.21875
- w_down: bfloat16 [3072, 768], P('mp', 'batch'), may hold values from -0.109375 to 0.109375
- grad_out: bfloat16 [16384, 768], P(('batch', 'mp')), may hold values from -6 to 6
Outputs:
- layer_out: bfloat16 [16384, 768], P(('batch', 'mp'))
- grad_tokens: float32 [16384, 768], P(('batch', 'mp'))
- grad_gain_attn: float32 [768], P(('mp', 'batch'))
- grad_gain_ffn: float32 [768], P(('mp', 'batch'))
- grad_w_qkv: float32 [768, 3, 768], P('batch', None, 'mp')
- grad_dconv: float32 [3, 3, 768], P(None, None, ('mp', 'batch'))
- grad_w_out: float32 [768, 768], P('mp', 'batch')
- grad_w_up: float32 [768, 3072], P('batch', 'mp')
- grad_w_down: float32 [3072, 768], P('mp', 'batch')
Inputs may be any that keep to these rules, and one draw needn't show every extreme that they name: `counts`: slots below a batch index's count are filled, the rest are empty; in every draw some batch index is full and some batch index holds a single sequence of exactly 128 slots. `seg_ids`: within a block of 2048 slots the ids never fall; each id of filled slots marks one sequence of 128 to 256 slots, except that a block's last sequence may be cut at the block's end; empty slots carry the id 2048 // 128 + 1, and some block has empty slots in every draw.
All inputs are finite; a program needn't handle non-finite values.
Results may differ from a plain program's by a relative error of at most 0.015.
Values may be sent and summed in bfloat16 or wider, within the bound.
A program may use at most 128 MiB of HBM per device.

v0:
```python
import jax
import jax.numpy as jnp
from jax import lax
from jax.sharding import PartitionSpec as P

HD = 64
SEQ_MAX = 256


EPSILON = 1e-06
MASKED = -1e30


def rms_norm(values, gains):
    return values * lax.rsqrt(jnp.mean(values * values, axis=-1, keepdims=True) + EPSILON) * gains


def shifted(values, offset_by, filler):
    leading = jnp.full((offset_by,) + values.shape[1:], filler, values.dtype)
    return jnp.concatenate([leading, values[:-offset_by]], axis=0)


def same_masks(segment):
    same_one = (segment == shifted(segment, 1, -1)).astype(jnp.float32)[:, None, None]
    same_two = (segment == shifted(segment, 2, -1)).astype(jnp.float32)[:, None, None]
    return (same_one, same_two)


def depthwise(projected, kernel, same_one, same_two):
    return (
        kernel[None, :, 0, :] * projected
        + kernel[None, :, 1, :] * shifted(projected, 1, 0.0) * same_one
        + kernel[None, :, 2, :] * shifted(projected, 2, 0.0) * same_two
    )


def inner_rows(left, right):
    return lax.dot_general(
        left, right, (((0,), (0,)), ((), ())), preferred_element_type=jnp.float32
    )


def against(left, right):
    return lax.dot_general(
        left, right, (((1,), (1,)), ((), ())), preferred_element_type=jnp.float32
    )


def padded_inputs(keys_all, values_all, segment):
    back_rows = SEQ_MAX
    keys_pad = jnp.concatenate(
        [jnp.zeros((back_rows,) + keys_all.shape[1:], keys_all.dtype), keys_all], axis=0
    )
    values_pad = jnp.concatenate(
        [jnp.zeros((back_rows,) + values_all.shape[1:], values_all.dtype), values_all], axis=0
    )
    segment_pad = jnp.concatenate([jnp.full((back_rows,), -1, jnp.int32), segment])
    return (keys_pad, values_pad, segment_pad)


def window_scores(queries, keys_pad, values_pad, segment_pad, offset, block_rows):
    back_rows = SEQ_MAX
    scaling = queries.shape[-1] ** (-0.5)
    q_block = lax.dynamic_slice_in_dim(queries, offset, block_rows, 0)
    k_block = lax.dynamic_slice_in_dim(keys_pad, offset, block_rows + back_rows, 0)
    v_block = lax.dynamic_slice_in_dim(values_pad, offset, block_rows + back_rows, 0)
    seg_query = lax.dynamic_slice_in_dim(segment_pad, offset + back_rows, block_rows, 0)
    seg_key = lax.dynamic_slice_in_dim(segment_pad, offset, block_rows + back_rows, 0)
    pos_query = offset + lax.iota(jnp.int32, block_rows)
    pos_key = offset - back_rows + lax.iota(jnp.int32, block_rows + back_rows)
    allowed = (seg_query[:, None] == seg_key[None, :]) & (pos_key[None, :] <= pos_query[:, None])
    scores = (
        jnp.einsum("qhd,khd->hqk", q_block, k_block, preferred_element_type=jnp.float32) * scaling
    )
    return (q_block, k_block, v_block, jnp.where(allowed[None], scores, MASKED))


def attend(queries, keys_all, values_all, segment):
    row_count = queries.shape[0]
    block_rows = min(512, row_count)
    keys_pad, values_pad, segment_pad = padded_inputs(keys_all, values_all, segment)

    def one_block(offset):
        q_block, k_block, v_block, scores = window_scores(
            queries, keys_pad, values_pad, segment_pad, offset, block_rows
        )
        row_max = jnp.max(scores, axis=-1, keepdims=True)
        expo = jnp.exp(scores - row_max)
        row_sum = jnp.sum(expo, axis=-1, keepdims=True)
        attn_prob = (expo / row_sum).astype(jnp.bfloat16)
        outputs = jnp.einsum("hqk,khd->qhd", attn_prob, v_block, preferred_element_type=jnp.float32)
        return (outputs, (row_max + jnp.log(row_sum))[..., 0])

    offsets = lax.iota(jnp.int32, row_count // block_rows) * block_rows
    outputs, log_norm = lax.map(one_block, offsets)
    return (outputs.reshape(row_count, queries.shape[1], queries.shape[2]), log_norm)


def attend_back(queries, keys_all, values_all, segment, log_norm, grad_heads):
    row_count = queries.shape[0]
    block_rows = min(512, row_count)
    back_rows = SEQ_MAX
    scaling = queries.shape[-1] ** (-0.5)
    keys_pad, values_pad, segment_pad = padded_inputs(keys_all, values_all, segment)

    def one_block(running, entry):
        offset, norm_block = entry
        grad_keys, grad_values = running
        q_block, k_block, v_block, scores = window_scores(
            queries, keys_pad, values_pad, segment_pad, offset, block_rows
        )
        attn_prob = jnp.exp(scores - norm_block[..., None])
        prob_low = attn_prob.astype(jnp.bfloat16)
        grad_block = lax.dynamic_slice_in_dim(grad_heads, offset, block_rows, 0)
        grad_prob = jnp.einsum(
            "qhd,khd->hqk", grad_block, v_block, preferred_element_type=jnp.float32
        )
        grad_scores = (
            attn_prob * (grad_prob - jnp.sum(attn_prob * grad_prob, axis=-1, keepdims=True))
        ).astype(jnp.bfloat16)
        grad_query = (
            jnp.einsum("hqk,khd->qhd", grad_scores, k_block, preferred_element_type=jnp.float32)
            * scaling
        )
        grad_key = (
            jnp.einsum("hqk,qhd->khd", grad_scores, q_block, preferred_element_type=jnp.float32)
            * scaling
        )
        grad_value = jnp.einsum(
            "hqk,qhd->khd", prob_low, grad_block, preferred_element_type=jnp.float32
        )
        span = block_rows + back_rows
        grad_keys = lax.dynamic_update_slice_in_dim(
            grad_keys, lax.dynamic_slice_in_dim(grad_keys, offset, span, 0) + grad_key, offset, 0
        )
        grad_values = lax.dynamic_update_slice_in_dim(
            grad_values,
            lax.dynamic_slice_in_dim(grad_values, offset, span, 0) + grad_value,
            offset,
            0,
        )
        return ((grad_keys, grad_values), grad_query)

    zeros_pad = jnp.zeros((row_count + back_rows,) + keys_all.shape[1:], jnp.float32)
    offsets = lax.iota(jnp.int32, row_count // block_rows) * block_rows
    (grad_keys, grad_values), grad_query = lax.scan(
        one_block, (zeros_pad, zeros_pad), (offsets, log_norm)
    )
    grad_query = grad_query.reshape(row_count, queries.shape[1], queries.shape[2])
    return (grad_query, grad_keys[back_rows:], grad_values[back_rows:])


def shards(
    tokens, seg_ids, counts, gain_attn, gain_ffn, w_qkv, dconv_kernel, w_out, w_up, w_down, grad_out
):
    share_rows = tokens.shape[0]
    row_count = seg_ids.shape[0]
    filled = (lax.iota(jnp.int32, row_count) < counts[0]).astype(jnp.float32)[:, None]
    own_start = lax.axis_index("mp") * share_rows
    own_filled = lax.dynamic_slice_in_dim(filled, own_start, share_rows, 0)
    same_one, same_two = same_masks(seg_ids)
    full_qkv, full_out, full_up, full_down = (
        lax.all_gather(w_qkv, "batch", axis=0, tiled=True),
        lax.all_gather(w_out, "batch", axis=1, tiled=True),
        lax.all_gather(w_up, "batch", axis=0, tiled=True),
        lax.all_gather(w_down, "batch", axis=1, tiled=True),
    )
    tok_full = lax.all_gather(tokens, "mp", axis=0, tiled=True).astype(jnp.float32)
    normed_float, norm_back_in = jax.vjp(rms_norm, tok_full, gain_attn)
    normed = normed_float.astype(jnp.bfloat16)
    projected = jnp.einsum("td,dgc->tgc", normed, full_qkv, preferred_element_type=jnp.float32)
    mixed_float, conv_back = jax.vjp(
        lambda source, kernel: depthwise(source, kernel, same_one, same_two),
        projected,
        dconv_kernel,
    )
    mixed_qkv = mixed_float.astype(jnp.bfloat16).reshape(row_count, 3, -1, HD)
    queries, keys_all, values_all = (mixed_qkv[:, 0], mixed_qkv[:, 1], mixed_qkv[:, 2])
    heads_float, log_norm = attend(queries, keys_all, values_all, seg_ids)
    heads_out = heads_float.reshape(row_count, -1).astype(jnp.bfloat16)
    attn_part = jnp.dot(heads_out, full_out, preferred_element_type=jnp.float32)
    attn_branch = lax.psum_scatter(attn_part, "mp", scatter_dimension=0, tiled=True)
    residual = tokens.astype(jnp.float32) + own_filled * attn_branch
    resid_full = lax.all_gather(residual, "mp", axis=0, tiled=True)
    normed_two_float, norm_back_mid = jax.vjp(rms_norm, resid_full, gain_ffn)
    normed_two = normed_two_float.astype(jnp.bfloat16)
    up_proj = jnp.dot(normed_two, full_up, preferred_element_type=jnp.float32)
    hidden = jnp.square(jax.nn.relu(up_proj)).astype(jnp.bfloat16)
    ffn_part = jnp.dot(hidden, full_down, preferred_element_type=jnp.float32)
    ffn_branch = lax.psum_scatter(
        ffn_part.astype(jnp.bfloat16), "mp", scatter_dimension=0, tiled=True
    ).astype(jnp.float32)
    layer_out = (residual + own_filled * ffn_branch).astype(jnp.bfloat16)
    full_qkv, full_out, full_up, full_down = (
        lax.all_gather(w_qkv, "batch", axis=0, tiled=True),
        lax.all_gather(w_out, "batch", axis=1, tiled=True),
        lax.all_gather(w_up, "batch", axis=0, tiled=True),
        lax.all_gather(w_down, "batch", axis=1, tiled=True),
    )
    grad_ffn = (own_filled * grad_out.astype(jnp.float32)).astype(jnp.bfloat16)
    grad_ffn_full = lax.all_gather(grad_ffn, "mp", axis=0, tiled=True)
    grad_w_down = inner_rows(hidden, grad_ffn_full)
    grad_up = (against(grad_ffn_full, full_down) * 2.0 * jax.nn.relu(up_proj)).astype(jnp.bfloat16)
    grad_w_up = inner_rows(normed_two, grad_up)
    grad_normed_two = against(grad_up, full_up)
    part_resid, part_gain_ffn = norm_back_mid(grad_normed_two)
    grad_mid, gain_ffn_share = (
        lax.psum_scatter(part_resid, "mp", scatter_dimension=0, tiled=True),
        lax.psum_scatter(part_gain_ffn, "mp", scatter_dimension=0, tiled=True),
    )
    grad_resid = grad_out.astype(jnp.float32) + grad_mid
    grad_attn = (own_filled * grad_resid).astype(jnp.bfloat16)
    grad_attn_full = lax.all_gather(grad_attn, "mp", axis=0, tiled=True)
    grad_w_out = inner_rows(heads_out, grad_attn_full)
    grad_heads = against(grad_attn_full, full_out).astype(jnp.bfloat16).reshape(row_count, -1, HD)
    grad_query, grad_key, grad_value = attend_back(
        queries, keys_all, values_all, seg_ids, log_norm, grad_heads
    )
    grad_mixed = jnp.stack([grad_query, grad_key, grad_value], axis=1).reshape(row_count, 3, -1)
    grad_proj_float, grad_dconv_part = conv_back(grad_mixed)
    grad_proj = grad_proj_float.astype(jnp.bfloat16)
    grad_w_qkv = jnp.einsum("td,tgc->dgc", normed, grad_proj, preferred_element_type=jnp.float32)
    grad_normed = jnp.einsum("tgc,dgc->td", grad_proj, full_qkv, preferred_element_type=jnp.float32)
    part_tokens, part_gain_attn = norm_back_in(grad_normed)
    grad_in_share, gain_attn_share = (
        lax.psum_scatter(
            part_tokens.astype(jnp.bfloat16), "mp", scatter_dimension=0, tiled=True
        ).astype(jnp.float32),
        lax.psum_scatter(
            part_gain_attn.astype(jnp.bfloat16), "mp", scatter_dimension=0, tiled=True
        ).astype(jnp.float32),
    )
    grad_tokens = grad_resid + grad_in_share
    summed = (
        lax.psum_scatter(grad_w_qkv, "batch", scatter_dimension=0, tiled=True),
        lax.psum_scatter(grad_w_out, "batch", scatter_dimension=1, tiled=True),
        lax.psum_scatter(grad_w_up, "batch", scatter_dimension=0, tiled=True),
        lax.psum_scatter(grad_w_down, "batch", scatter_dimension=1, tiled=True),
        lax.psum_scatter(grad_dconv_part, "batch", scatter_dimension=2, tiled=True),
        lax.psum_scatter(gain_attn_share, "batch", scatter_dimension=0, tiled=True),
        lax.psum_scatter(gain_ffn_share, "batch", scatter_dimension=0, tiled=True),
    )
    return (
        layer_out,
        grad_tokens,
        summed[5],
        summed[6],
        summed[0],
        summed[4],
        summed[1],
        summed[2],
        summed[3],
    )


def solution(mesh):
    in_specs = (
        P(("batch", "mp"), None),
        P("batch"),
        P("batch"),
        P(),
        P(),
        P("batch", None, "mp"),
        P(None, None, "mp"),
        P("mp", "batch"),
        P("batch", "mp"),
        P("mp", "batch"),
        P(("batch", "mp"), None),
    )
    out_specs = (
        P(("batch", "mp"), None),
        P(("batch", "mp"), None),
        P(("mp", "batch")),
        P(("mp", "batch")),
        P("batch", None, "mp"),
        P(None, None, ("mp", "batch")),
        P("mp", "batch"),
        P("batch", "mp"),
        P("mp", "batch"),
    )
    return jax.shard_map(shards, mesh=mesh, in_specs=in_specs, out_specs=out_specs, check_vma=False)
```

profile of v0, /device:TPU:0, one launch (start us, length us, event | category | flops | bytes accessed | tf_op | source)
XLA Modules:
  0.0 958.3 jit_solution(17018985462925140918)
XLA Ops:
  10.8 38.7 %all_gather.29 = bf16[768,3,192]{2,1,0:T(4,128)(2,1)S(1)} all-gather(bf16[96,3,192]{2,1,0:T(4,128)(2,1)S(1)} %copy.30), channel_id=1, replica_groups=mesh['mp'=4,'batch'=8] {'batch'}, dimensions={0}, use_global_device_ids=true | all-gather | bytes 995328 | tf_op jit(solution)/shard_map/all_gather | solution.py:163
  50.4 33.1 %all_gather.30 = bf16[192,768]{0,1:T(8,128)(2,1)} all-gather(bf16[192,96]{0,1:T(8,128)(2,1)S(1)} %copy.33), channel_id=1, replica_groups=mesh['mp'=4,'batch'=8] {'batch'}, dimensions={1}, use_global_device_ids=true | all-gather | bytes 331776 | tf_op jit(solution)/shard_map/all_gather | solution.py:164
  86.3 4.0 fusion.53
  90.4 3.7 add_convert_fusion.1
  94.5 45.9 %while.30 = (s32[]{:T(128)}, bf16[4,512,3,64]{1,3,2,0:T(8,128)(2,1)S(1)}, f32[4,3,512]{2,1,0:T(4,128)S(1)}, s32[4]{0:T(128)S(1)}, bf16[2304,3,64]{0,2,1:T(8,128)...) while((s32[]{:T(128)}, ...), condition=%wide.region_4.5_spmd, body=%wide.region_1.4_spmd.sunk | while | flops 317325056 | bytes 16993592 | solution.py:95
  141.4 4.7 fusion.66
  146.9 57.2 %reduce-scatter.12.cloned.1.call-done = f32[512,768]{1,0:T(8,128)} async-done(((f32[2048,768]{1,0:T(8,128)}), f32[512,768]{1,0:T(8,128)}) %reduce-scatter.12.cloned.1.call-update) | async-done | bytes 1572880 | tf_op jit(solution)/shard_map/reduce_scatter | solution.py:182
  209.5 44.5 %all-gather.9.cloned.1.call-done = f32[2048,768]{1,0:T(8,128)} async-done(((f32[512,768]{1,0:T(8,128)}), f32[2048,768]{1,0:T(8,128)}) %all-gather.9.cloned.1.call-update) | async-done | bytes 6291472 | tf_op jit(solution)/shard_map/all_gather | solution.py:184
  257.2 39.9 %all-gather.11.cloned.1.call-done = bf16[768,768]{1,0:T(8,128)(2,1)} async-done(((bf16[96,768]{1,0:T(8,128)(2,1)}), bf16[768,768]{1,0:T(8,128)(2,1)}) %all-gather.11.cloned.1.call-update) | async-done | bytes 1179664 | tf_op jit(solution)/shard_map/all_gather | solution.py:165
  297.2 8.4 fusion.64
  305.6 33.5 %all-gather.13.cloned.1.call-done = bf16[768,768]{0,1:T(8,128)(2,1)} async-done(((bf16[768,96]{0,1:T(8,128)(2,1)}), bf16[768,768]{0,1:T(8,128)(2,1)}) %all-gather.13.cloned.1.call-update) | async-done | bytes 1179664 | tf_op jit(solution)/shard_map/all_gather | solution.py:166
  339.0 7.4 convolution_convert_fusion
  346.5 21.8 %all-gather.15.cloned.1.call-done = bf16[2048,768]{1,0:T(8,128)(2,1)} async-done(((bf16[512,768]{1,0:T(8,128)(2,1)}), bf16[2048,768]{1,0:T(8,128)(2,1)}) %all-gather.15.cloned.1.call-update) | async-done | bytes 3145744 | tf_op jit(solution)/shard_map/all_gather | solution.py:201
  368.2 6.9 multiply_convert_fusion.1
  375.2 6.7 multiply_reduce_fusion.1
  385.3 23.4 %reduce-scatter.14.cloned.1.call-done = bf16[512,768]{1,0:T(8,128)(2,1)} async-done(((bf16[2048,768]{1,0:T(8,128)(2,1)}), bf16[512,768]{1,0:T(8,128)(2,1)}) %reduce-scatter.14.cloned.1.call-update) | async-done | bytes 786448 | tf_op jit(solution)/shard_map/reduce_scatter | solution.py:190
  408.7 61.4 %reduce-scatter.16.cloned.1.call-done = f32[512,768]{1,0:T(8,128)} async-done(((f32[2048,768]{1,0:T(8,128)}), f32[512,768]{1,0:T(8,128)}) %reduce-scatter.16.cloned.1.call-update) | async-done | bytes 1572880 | tf_op jit(solution)/shard_map/reduce_scatter | solution.py:208
  470.1 3.6 multiply_convert_fusion.4
  473.8 28.6 %all-gather.17.cloned.1.call-done = bf16[2048,768]{1,0:T(8,128)(2,1)} async-done(((bf16[512,768]{1,0:T(8,128)(2,1)}), bf16[2048,768]{1,0:T(8,128)(2,1)}) %all-gather.17.cloned.1.call-update) | async-done | bytes 3145744 | tf_op jit(solution)/shard_map/all_gather | solution.py:213
  502.4 4.1 convolution_bitcast_fusion
  506.5 9.0 reduce-scatter.18.cloned.1.call-start
  515.6 4.0 convolution_convert_fusion.1
  522.3 149.0 %while.31 = (s32[]{:T(128)}, f32[2304,3,64]{0,2,1:T(8,128)}, f32[2304,3,64]{0,2,1:T(8,128)}, f32[4,512,3,64]{1,0,3,2:T(4,128)}, s32[4]{0:T(128)S(1)}, /*index=5*...) while((s32[]{:T(128)}, f32[2304,3,64]{0,2,1:T(8,128)}, ...), condition=%wide.region_12.13_spmd, body=%wide.region_10.12_spmd.sunk | while | flops 774389504 | bytes 78417336 | solution.py:146
  535.1 3.6 dynamic_update_slice.42
  538.7 4.7 multiply_reduce_fusion.8
  547.8 8.6 dynamic_update_slice.43
  556.4 3.5 dynamic_update_slice.41
  572.7 3.6 dynamic_update_slice.42
  576.3 4.7 multiply_reduce_fusion.8
  585.4 8.6 dynamic_update_slice.43
  594.0 3.5 dynamic_update_slice.41
  610.4 3.5 dynamic_update_slice.42
  613.9 4.7 multiply_reduce_fusion.8
  623.0 8.6 dynamic_update_slice.43
  631.6 3.5 dynamic_update_slice.41
  650.7 4.7 multiply_reduce_fusion.8
  659.7 8.6 dynamic_update_slice.43
  676.6 5.5 multiply_reduce_fusion.6
  687.0 3.7 fusion.45
  693.5 6.9 fusion.55
  700.6 9.1 fusion.63
  709.8 6.4 fusion.49
  718.7 6.8 all-reduce.13
  725.5 6.2 all-reduce.11
  731.8 37.7 %all-reduce.16 = (f32[192]{0:T(256)S(1)}, f32[192]{0:T(256)S(1)}, f32[3,3,192]{2,0,1:T(4,128)S(1)}) all-reduce(f32[192]{0:T(256)S(1)} %dynamic-slice_convert_fusion, f32[192]{0:T(256)S(1)} %dynamic-slice.9, f32[3,3,192]{2,0,1:T(4,128)S(1)} %pad_add_fusion), channel_id=7, replica_groups=mesh['mp'=4,'batch'=8] {'batch'}, use_global_device_ids=true, to_apply=%region_17.18.clone | all-reduce | flops 2112 | bytes 16896
  776.1 29.4 %reduce-scatter.24.cloned.1.call-done = f32[768,96]{0,1:T(8,128)} async-done(((f32[768,768]{0,1:T(8,128)}), f32[768,96]{0,1:T(8,128)}) %reduce-scatter.24.cloned.1.call-update) | async-done | bytes 294928 | tf_op jit(solution)/shard_map/reduce_scatter | solution.py:238
  805.5 73.1 %reduce-scatter.22.cloned.1.call-done = f32[96,768]{1,0:T(8,128)} async-done(((f32[768,768]{1,0:T(8,128)}), f32[96,768]{1,0:T(8,128)}) %reduce-scatter.22.cloned.1.call-update) | async-done | bytes 294928 | tf_op jit(solution)/shard_map/reduce_scatter | solution.py:237
  878.6 72.7 %reduce-scatter.20.cloned.1.call-done = f32[96,3,192]{2,0,1:T(8,128)} async-done(((f32[768,3,192]{2,0,1:T(8,128)}), f32[96,3,192]{2,0,1:T(8,128)}) %reduce-scatter.20.cloned.1.call-update) | async-done | bytes 221200 | tf_op jit(solution)/shard_map/reduce_scatter | solution.py:235
  (271 shorter events, 122.9 us)
Async XLA Ops:
  7.2 43.2 %copy-start.12 = (s32[2048]{0:T(1024)S(1)}, s32[2048]{0:T(1024)}, u32[]{:S(2)}) copy-start(s32[2048]{0:T(1024)} %param.16) | copy-start | bytes 24580
  7.2 79.2 %copy-start.28 = (f32[768]{0:T(1024)S(1)}, f32[768]{0:T(1024)}, u32[]{:S(2)}) copy-start(f32[768]{0:T(1024)} %param.18) | copy-start | bytes 9220
  7.2 76.5 %all-gather.7.cloned.1.call-start = ((), (), s32[]{:S(2)}) async-start(), calls=%async_computation.8 | async-start | bytes 3932160 | tf_op jit(solution)/shard_map/all_gather | solution.py:168
  7.9 196.1 %reduce-scatter.12.cloned.1.call-start = ((), (), s32[]{:S(2)}) async-start(), calls=%async_computation.9 | async-start | bytes 7864320 | tf_op jit(solution)/shard_map/reduce_scatter | solution.py:182
  8.8 81.5 %copy-start.19 = (f32[3,1,192]{2,0,1:T(4,128)}, f32[3,1,192]{2,0,1:T(4,128)S(1)}, u32[]{:S(2)}) copy-start(f32[3,1,192]{2,0,1:T(4,128)S(1)} %copy.69) | copy-start | bytes 6916
  50.4 39.9 %copy-start.10 = (bf16[768,3,192]{0,2,1:T(8,128)(2,1)}, bf16[768,3,192]{0,2,1:T(8,128)(2,1)S(1)}, u32[]{:S(2)}) copy-start(bf16[768,3,192]{0,2,1:T(8,128)(2,1)S(1)} %copy.31) | copy-start | bytes 2654212
  83.6 6.8 copy-start.21
  83.6 6.8 copy-start.23
  83.7 6.7 copy-start.15
  83.7 6.7 copy-start.17
  86.3 4.1 copy-start.13
  86.3 4.0 copy-start.25
  90.4 3.7 copy-start.1
  146.1 58.0 %copy-start.5 = (bf16[512,768]{1,0:T(8,128)(2,1)S(1)}, bf16[512,768]{1,0:T(8,128)(2,1)}, u32[]{:S(2)}) copy-start(bf16[512,768]{1,0:T(8,128)(2,1)} %param.25) | copy-start | bytes 2359300
  146.1 107.9 %all-gather.9.cloned.1.call-start = ((), (), s32[]{:S(2)}) async-start(), calls=%async_computation.10 | async-start | bytes 7864320 | tf_op jit(solution)/shard_map/all_gather | solution.py:184
  207.4 89.7 %copy-start.27 = (f32[768]{0:T(1024)S(1)}, f32[768]{0:T(1024)}, u32[]{:S(2)}) copy-start(f32[768]{0:T(1024)} %param.19) | copy-start | bytes 9220
  207.5 89.7 %all-gather.11.cloned.1.call-start = ((), (), s32[]{:S(2)}) async-start(), calls=%async_computation.11 | async-start | bytes 1327104 | tf_op jit(solution)/shard_map/all_gather | solution.py:165
  208.0 131.0 %all-gather.13.cloned.1.call-start = ((), (), s32[]{:S(2)}) async-start(), calls=%async_computation.12 | async-start | bytes 1327104 | tf_op jit(solution)/shard_map/all_gather | solution.py:166
  208.6 159.6 %all-gather.15.cloned.1.call-start = ((), (), s32[]{:S(2)}) async-start(), calls=%async_computation.14 | async-start | bytes 3932160 | tf_op jit(solution)/shard_map/all_gather | solution.py:201
  209.2 199.5 %reduce-scatter.14.cloned.1.call-start = ((), (), s32[]{:S(2)}) async-start(), calls=%async_computation.13 | async-start | bytes 3932160 | tf_op jit(solution)/shard_map/reduce_scatter | solution.py:190
  346.4 123.7 %reduce-scatter.16.cloned.1.call-start = ((), (), s32[]{:S(2)}) async-start(), calls=%async_computation.15 | async-start | bytes 7864320 | tf_op jit(solution)/shard_map/reduce_scatter | solution.py:208
  368.2 6.9 copy-start.31
  368.2 13.7 %slice-start.2 = ((s8[6291456]{0:T(1024)(128)(4,1)}), s8[4194304]{0:T(1024)(128)(4,1)S(1)}, s32[]{:S(2)}) async-start(s8[6291456]{0:T(1024)(128)(4,1)} %bitcast.126), calls=%async_computation.24 | async-start | bytes 8388608
  375.2 6.8 copy-start.34
  375.2 6.8 slice-start.3
  385.3 117.1 %all-gather.17.cloned.1.call-start = ((), (), s32[]{:S(2)}) async-start(), calls=%async_computation.16 | async-start | bytes 3932160 | tf_op jit(solution)/shard_map/all_gather | solution.py:213
  473.7 41.9 %copy-start.8 = (bf16[192,768]{0,1:T(8,128)(2,1)S(1)}, bf16[192,768]{0,1:T(8,128)(2,1)}, u32[]{:S(2)}) copy-start(bf16[192,768]{0,1:T(8,128)(2,1)} %all_gather.30) | copy-start | bytes 884740
  473.7 297.5 %reduce-scatter.26.cloned.1.call-start = ((), (), s32[]{:S(2)}) async-start(), calls=%async_computation.21 | async-start | bytes 884736
  506.5 266.4 %reduce-scatter.18.cloned.1.call-start = ((), (), s32[]{:S(2)}) async-start(), calls=%async_computation.17 | async-start | bytes 3932160 | tf_op jit(solution)/shard_map/reduce_scatter | solution.py:226
  535.1 8.3 slice-start
  538.7 4.7 slice-start.1
  572.7 8.4 slice-start
  576.3 4.7 slice-start.1
  610.3 8.3 slice-start
  613.9 4.7 slice-start.1
  647.8 7.6 slice-start
  650.7 4.7 slice-start.1
  671.3 4.2 copy-start.6
  671.3 4.4 copy-start.16
  671.3 4.4 copy-start.18
  676.6 5.5 copy-start.24
  687.0 3.7 copy-start.14
  693.4 112.1 %reduce-scatter.24.cloned.1.call-start = ((), (), s32[]{:S(2)}) async-start(), calls=%async_computation.20 | async-start | bytes 2654208 | tf_op jit(solution)/shard_map/reduce_scatter | solution.py:238
  700.3 9.5 copy-start.4
  700.3 178.3 %reduce-scatter.22.cloned.1.call-start = ((), (), s32[]{:S(2)}) async-start(), calls=%async_computation.19 | async-start | bytes 2654208 | tf_op jit(solution)/shard_map/reduce_scatter | solution.py:237
  709.7 6.5 copy-start.33
  709.7 7.1 copy-start.32
  709.7 241.6 %reduce-scatter.20.cloned.1.call-start = ((), (), s32[]{:S(2)}) async-start(), calls=%async_computation.18 | async-start | bytes 2654208 | tf_op jit(solution)/shard_map/reduce_scatter | solution.py:235
  (14 other events, 29.5 us)
Sparse Core Ops, SparseCore 0:
  9.6 31.2 all-gather.6
  146.2 57.8 reduce-scatter.11
  207.6 46.3 all-gather.8
  256.0 41.1 all-gather.10
  299.2 39.7 all-gather.12
  341.0 27.1 all-gather.14
  370.8 37.8 reduce-scatter.13
  411.2 58.8 reduce-scatter.15
  473.9 28.4 all-gather.16
  506.7 63.3 reduce-scatter.25
  693.5 38.0 reduce-scatter.17
  735.6 69.8 reduce-scatter.23
  809.6 68.9 reduce-scatter.21
  882.5 68.7 reduce-scatter.19
where the time goes:
time: 970 us; the launch traced here: 958 us
  waiting for transfers between devices  488 us (50%)
  matrix products  129 us (13%)
  blocking collectives  122 us (13%)
  local copies, waits for them, and re-layouts  96.4 us (10%)
  other arithmetic  53.5 us (6%)
  loops' own time  41.9 us (4%)
  between operations  17.1 us (2%)
  starting transfers between devices  10.1 us (1%)
    reduce_scatter x1, waiting for transfers between devices, shards(): lax.psum_scatter(grad_w_up, 'batch', scatter_dimension=0, tiled=True)  73.1 us
    reduce_scatter x1, waiting for transfers between devices, shards(): lax.psum_scatter(grad_w_qkv, 'batch', scatter_dimension=0, tiled=True)  72.7 us
    reduce_scatter x1, waiting for transfers between devices, shards(): lax.psum_scatter(part_resid, 'mp', scatter_dimension=0, tiled=True)  61.4 us
    reduce_scatter x1, waiting for transfers between devices, shards(): lax.psum_scatter(attn_part, 'mp', scatter_dimension=0, tiled=True)  57.2 us
    unnamed x3, blocking collectives  50.6 us
    all_gather x1, waiting for transfers between devices, shards(): resid_full = lax.all_gather(residual, 'mp', axis=0, tiled=True)  44.5 us
    all_gather x1, waiting for transfers between devices, shards(): lax.all_gather(w_up, 'batch', axis=0, tiled=True)  39.9 us
    all_gather x1, blocking collectives, shards(): lax.all_gather(w_qkv, 'batch', axis=0, tiled=True)  38.7 us
  transfers between devices with their start and end apart: 14, of which 11 were waited for; matrix products, arithmetic and copies ran while one was open for 23% of the time, Pallas kernels for 0%

commit v1 on v0

v1 whole, which is shorter than its diff:
```python
import jax
import jax.numpy as jnp
from jax import lax
from jax.experimental import pallas as pl
from jax.experimental.pallas import tpu as pltpu
from jax.sharding import PartitionSpec as P

HD = 64
SEQ_MAX = 256
PAD = 16
EPSILON = 1e-06
MASKED = -1e30
F32 = jnp.float32
BF16 = jnp.bfloat16


def nt(left, right):
    return lax.dot_general(left, right, (((1,), (1,)), ((), ())), preferred_element_type=F32)


def nn(left, right):
    return lax.dot_general(left, right, (((1,), (0,)), ((), ())), preferred_element_type=F32)


def tn(left, right):
    return lax.dot_general(left, right, (((0,), (0,)), ((), ())), preferred_element_type=F32)


def head_mask(values, head):
    lane = lax.broadcasted_iota(jnp.int32, values.shape, 1)
    return jnp.where((lane >= head * HD) & (lane < (head + 1) * HD), values, jnp.zeros_like(values))


def attend_kernel(q_ref, k_ref, v_ref, seg_key_ref, seg_query_ref, out_ref, prob_ref, bias_ref):
    tile = SEQ_MAX
    tiles = q_ref.shape[0] // tile

    @pl.when(pl.program_id(0) == 0)
    def _():
        for at in range(tiles):
            key = lax.broadcasted_iota(jnp.int32, (2 * tile, tile), 0)
            query = lax.broadcasted_iota(jnp.int32, (2 * tile, tile), 1) + tile
            same = seg_key_ref[at * tile : (at + 2) * tile, :] == seg_query_ref[:, at * tile : (at + 1) * tile]
            bias_ref[at] = jnp.where(same & (key <= query), 0.0, MASKED).astype(F32)

    for at in range(tiles):
        keys = k_ref[at * tile : (at + 2) * tile, :]
        values = v_ref[at * tile : (at + 2) * tile, :]
        queries = q_ref[at * tile : (at + 1) * tile, :] * jnp.asarray(HD**-0.5, BF16)
        outs = []
        for head in range(2):
            scores = nt(keys, head_mask(queries, head)) + bias_ref[at]
            expo = jnp.exp(scores - jnp.max(scores, axis=0, keepdims=True))
            prob = (expo * (1.0 / jnp.sum(expo, axis=0, keepdims=True))).astype(BF16)
            prob_ref[0, at, head] = prob
            outs.append(tn(head_mask(values, head), prob))
        out_ref[at * tile : (at + 1) * tile, :] = (outs[0] + outs[1]).T.astype(BF16)


def attend_back_kernel(q_ref, k_ref, v_ref, grad_ref, prob_ref, dq_ref, dk_ref, dv_ref):
    tile = SEQ_MAX
    tiles = q_ref.shape[0] // tile
    dk_ref[...] = jnp.zeros_like(dk_ref)
    dv_ref[...] = jnp.zeros_like(dv_ref)
    for at in range(tiles):
        span = slice(at * tile, (at + 2) * tile)
        keys = k_ref[span, :]
        values = v_ref[span, :]
        queries = q_ref[at * tile : (at + 1) * tile, :] * jnp.asarray(HD**-0.5, BF16)
        grads = grad_ref[at * tile : (at + 1) * tile, :]
        dq = 0.0
        for head in range(2):
            prob = prob_ref[0, at, head]
            grad_head = head_mask(grads, head)
            grad_prob = nt(values, grad_head)
            wide = prob.astype(F32)
            inner = wide * grad_prob
            grad_scores = (inner - wide * jnp.sum(inner, axis=0, keepdims=True)).astype(BF16)
            dv_ref[span, :] += nn(prob, grad_head)
            dk_ref[span, :] += nn(grad_scores, head_mask(queries, head))
            dq = dq + tn(head_mask(keys, head), grad_scores)
        dq_ref[at * tile : (at + 1) * tile, :] = (dq * HD**-0.5).T


def attend(queries, keys, values, seg_key, seg_query):
    rows, width = queries.shape
    span = keys.shape[0]
    tiles = rows // SEQ_MAX
    wide = 2 * HD
    return pl.pallas_call(
        attend_kernel,
        grid=(width // wide,),
        in_specs=[
            pl.BlockSpec((rows, wide), lambda i: (0, i)),
            pl.BlockSpec((span, wide), lambda i: (0, i)),
            pl.BlockSpec((span, wide), lambda i: (0, i)),
            pl.BlockSpec((span, 1), lambda i: (0, 0)),
            pl.BlockSpec((1, rows), lambda i: (0, 0)),
        ],
        out_specs=[
            pl.BlockSpec((rows, wide), lambda i: (0, i)),
            pl.BlockSpec((1, tiles, 2, 2 * SEQ_MAX, SEQ_MAX), lambda i: (i, 0, 0, 0, 0)),
        ],
        out_shape=[
            jax.ShapeDtypeStruct((rows, width), BF16),
            jax.ShapeDtypeStruct((width // wide, tiles, 2, 2 * SEQ_MAX, SEQ_MAX), BF16),
        ],
        scratch_shapes=[pltpu.VMEM((tiles, 2 * SEQ_MAX, SEQ_MAX), F32)],
        name="attend",
    )(queries, keys, values, seg_key[:, None], seg_query[None, :])


def attend_back(queries, keys, values, grads, prob):
    rows, width = queries.shape
    span = keys.shape[0]
    tiles = rows // SEQ_MAX
    wide = 2 * HD
    return pl.pallas_call(
        attend_back_kernel,
        grid=(width // wide,),
        in_specs=[
            pl.BlockSpec((rows, wide), lambda i: (0, i)),
            pl.BlockSpec((span, wide), lambda i: (0, i)),
            pl.BlockSpec((span, wide), lambda i: (0, i)),
            pl.BlockSpec((rows, wide), lambda i: (0, i)),
            pl.BlockSpec((1, tiles, 2, 2 * SEQ_MAX, SEQ_MAX), lambda i: (i, 0, 0, 0, 0)),
        ],
        out_specs=[
            pl.BlockSpec((rows, wide), lambda i: (0, i)),
            pl.BlockSpec((span, wide), lambda i: (0, i)),
            pl.BlockSpec((span, wide), lambda i: (0, i)),
        ],
        out_shape=[
            jax.ShapeDtypeStruct((rows, width), F32),
            jax.ShapeDtypeStruct((span, width), F32),
            jax.ShapeDtypeStruct((span, width), F32),
        ],
        name="attend_back",
    )(queries, keys, values, grads, prob)


def rms(values):
    return lax.rsqrt(jnp.mean(values * values, axis=-1, keepdims=True) + EPSILON)


def rms_back(grad, gain, hat, scale):
    scaled = grad * gain
    return scale * (scaled - hat * jnp.mean(scaled * hat, axis=-1, keepdims=True))


def later(values, by):
    return jnp.concatenate([jnp.zeros((by,) + values.shape[1:], values.dtype), values[:-by]], axis=0)


def sooner(values, by):
    return jnp.concatenate([values[by:], jnp.zeros((by,) + values.shape[1:], values.dtype)], axis=0)


def shards(
    tokens, seg_ids, counts, gain_attn, gain_ffn, w_qkv, dconv_kernel, w_out, w_up, w_down, grad_out
):
    rows, width = tokens.shape
    halo = SEQ_MAX + PAD
    n_mp = lax.axis_size("mp")
    n_batch = lax.axis_size("batch")
    part = width // n_mp
    ff = w_up.shape[1] * n_mp
    own_start = lax.axis_index("mp") * rows

    packed = jnp.concatenate(
        [w_qkv.reshape(w_qkv.shape[0], -1), w_out.T, w_up, w_down.T], axis=1
    )
    full = lax.all_gather(packed, ("batch", "mp"), axis=0, tiled=False)
    full = full.reshape((n_batch, n_mp) + packed.shape).transpose(0, 2, 1, 3).reshape(width, n_mp, -1)
    cuts = (3 * part, 4 * part, 4 * part + w_up.shape[1])
    full_qkv = full[:, :, : cuts[0]].reshape(width, n_mp, 3, part).transpose(0, 2, 1, 3).reshape(width, 3 * width)
    full_out = full[:, :, cuts[0] : cuts[1]].reshape(width, width)
    full_up = full[:, :, cuts[1] : cuts[2]].reshape(width, ff)
    full_down = full[:, :, cuts[2] :].reshape(width, ff)
    kernel = lax.all_gather(dconv_kernel, "mp", axis=2, tiled=True).transpose(1, 0, 2).reshape(3, 3 * width)

    back = [(i, i + 1) for i in range(n_mp - 1)]
    tok_halo = lax.ppermute(tokens[rows - halo :], "mp", back)
    ext = jnp.concatenate([tok_halo, tokens], axis=0).astype(F32)
    seg_pad = jnp.concatenate([jnp.full((halo,), -1, jnp.int32), seg_ids])
    seg = lax.dynamic_slice_in_dim(seg_pad, own_start, halo + rows, 0)
    same_one = (seg == later(seg, 1)).astype(F32)[:, None]
    same_two = (seg == later(seg, 2)).astype(F32)[:, None]
    slot = own_start + lax.iota(jnp.int32, rows)
    filled = (slot < counts[0]).astype(F32)[:, None]

    scale_one = rms(ext)
    hat_one = ext * scale_one
    normed = (hat_one * gain_attn).astype(BF16)
    projected = nn(normed, full_qkv)
    mixed = (
        kernel[0] * projected
        + kernel[1] * same_one * later(projected, 1)
        + kernel[2] * same_two * later(projected, 2)
    ).astype(BF16)
    queries = mixed[halo:, :width]
    keys = mixed[PAD:, width : 2 * width]
    values = mixed[PAD:, 2 * width :]
    heads, prob = attend(queries, keys, values, seg[PAD:], seg[halo:])
    residual = ext[halo:] + filled * nn(heads, full_out.T if False else full_out.T)
    scale_two = rms(residual)
    hat_two = residual * scale_two
    normed_two = (hat_two * gain_ffn).astype(BF16)
    up = jax.nn.relu(nn(normed_two, full_up))
    hidden = (up * up).astype(BF16)
    layer_out = (residual + filled * nt(hidden, full_down)).astype(BF16)

    grad = grad_out.astype(F32)
    grad_ffn = (filled * grad).astype(BF16)
    grad_up = (nn(grad_ffn, full_down) * 2.0 * up).astype(BF16)
    grad_w_down = tn(grad_ffn, hidden)
    grad_w_up = tn(normed_two, grad_up)
    grad_normed_two = nt(grad_up, full_up)
    grad_resid = grad + rms_back(grad_normed_two, gain_ffn, hat_two, scale_two)
    grad_gain_ffn = jnp.sum(grad_normed_two * hat_two, axis=0)
    grad_attn = (filled * grad_resid).astype(BF16)
    grad_w_out = tn(grad_attn, heads)
    grad_heads = nn(grad_attn, full_out).astype(BF16)
    dq, dk, dv = attend_back(queries, keys, values, grad_heads, prob)
    grad_mixed = jnp.concatenate(
        [
            jnp.pad(dq, ((halo, 0), (0, 0))),
            jnp.pad(dk, ((PAD, 0), (0, 0))),
            jnp.pad(dv, ((PAD, 0), (0, 0))),
        ],
        axis=1,
    )
    one = grad_mixed * same_one
    two = grad_mixed * same_two
    grad_kernel = jnp.stack(
        [
            jnp.sum(grad_mixed * projected, axis=0),
            jnp.sum(one * later(projected, 1), axis=0),
            jnp.sum(two * later(projected, 2), axis=0),
        ]
    )
    grad_proj = (
        kernel[0] * grad_mixed + kernel[1] * sooner(one, 1) + kernel[2] * sooner(two, 2)
    ).astype(BF16)
    grad_w_qkv = tn(normed, grad_proj)
    grad_normed = nt(grad_proj, full_qkv)
    ahead = [(i + 1, i) for i in range(n_mp - 1)]
    passed = lax.ppermute(grad_normed[:halo].astype(BF16), "mp", ahead).astype(F32)
    own_normed = grad_normed[halo:] + jnp.pad(passed, ((rows - halo, 0), (0, 0)))
    grad_tokens = grad_resid + rms_back(own_normed, gain_attn, hat_one[halo:], scale_one[halo:])
    grad_gain_attn = jnp.sum(own_normed * hat_one[halo:], axis=0)

    shard = packed.shape[0]
    grads = jnp.concatenate(
        [
            grad_w_qkv.astype(BF16).reshape(width, 3, n_mp, part).transpose(0, 2, 1, 3).reshape(width, n_mp, -1),
            grad_w_out.astype(BF16).reshape(width, n_mp, -1),
            grad_w_up.astype(BF16).reshape(width, n_mp, -1),
            grad_w_down.astype(BF16).reshape(width, n_mp, -1),
        ],
        axis=2,
    )
    grads = grads.reshape(n_batch, shard, n_mp, -1).transpose(0, 2, 1, 3).reshape(n_batch * n_mp, shard, -1)
    own = lax.psum_scatter(grads, ("batch", "mp"), scatter_dimension=0, tiled=False).astype(F32)
    small = jnp.concatenate(
        [grad_kernel.reshape(3, 3, width).transpose(1, 0, 2).reshape(9, width), grad_gain_attn[None], grad_gain_ffn[None]]
    )
    piece = width // (n_mp * n_batch)
    small = small.reshape(11, n_mp * n_batch, piece).transpose(1, 0, 2)
    small = lax.psum_scatter(small, ("mp", "batch"), scatter_dimension=0, tiled=False)
    return (
        layer_out,
        grad_tokens,
        small[9],
        small[10],
        own[:, : cuts[0]].reshape(shard, 3, part),
        small[:9].reshape(3, 3, piece),
        own[:, cuts[0] : cuts[1]].T,
        own[:, cuts[1] : cuts[2]],
        own[:, cuts[2] :].T,
    )


def solution(mesh):
    in_specs = (
        P(("batch", "mp"), None),
        P("batch"),
        P("batch"),
        P(),
        P(),
        P("batch", None, "mp"),
        P(None, None, "mp"),
        P("mp", "batch"),
        P("batch", "mp"),
        P("mp", "batch"),
        P(("batch", "mp"), None),
    )
    out_specs = (
        P(("batch", "mp"), None),
        P(("batch", "mp"), None),
        P(("mp", "batch")),
        P(("mp", "batch")),
        P("batch", None, "mp"),
        P(None, None, ("mp", "batch")),
        P("mp", "batch"),
        P("batch", "mp"),
        P("mp", "batch"),
    )
    return jax.shard_map(shards, mesh=mesh, in_specs=in_specs, out_specs=out_specs, check_vma=False)
```

time: 970 us -> 601 us (0.62)
  waiting for transfers between devices: 488 us -> 208 us
  local copies, waits for them, and re-layouts: 96.4 us -> 201 us
  matrix products: 129 us -> 40.8 us
  blocking collectives: 122 us -> 62.5 us
  loops' own time: 41.9 us -> 0 us
  Pallas kernels: 0 us -> 24.4 us
  other arithmetic: 53.5 us -> 37.4 us
    reduce_scatter x7 -> x1, waiting for transfers between devices: 317 us -> 136 us  [shards(): lax.psum_scatter(grads, ('batch', 'mp'), scatter_dimension=0, tiled=False)]
    all_gather x6 -> x1, waiting for transfers between devices: 168 us -> 71.9 us  [shards(): full = lax.all_gather(packed, ('batch', 'mp'), axis=0, tiled=False)]
    concatenate x3 -> x10, local copies, waits for them, and re-layouts: 0.14 us -> 85.8 us  [the longest x6 83.7 us: shards(): jnp.concatenate([grad_w_qkv.astype(BF16).reshape(width, 3, n_mp, part).tr...]
    dot_general x38 -> x12, matrix products: 121 us -> 40.8 us  [the longest x4 15.4 us: tn(): lax.dot_general(left, right, (((0,), (0,)), ((), ())), preferred_element_...]
    dynamic_update_slice x16 -> x0, local copies, waits for them, and re-layouts: 63.2 us -> none  [the longest x8 36.1 us: attend(): outputs, log_norm = lax.map(one_block, offsets)]
    all_gather x2 -> x1, blocking collectives: 71.9 us -> 17.1 us  [shards(): lax.all_gather(dconv_kernel, 'mp', axis=2, tiled=True).transpose(1, 0, 2)]
    slice x3 -> x22, local copies, waits for them, and re-layouts: 2.67 us -> 51.5 us  [the longest x2 14.7 us: shards(): full_up = full[:, :, cuts[1]:cuts[2]].reshape(width, ff)]
    another operation x2 -> x0, loops' own time: 41.9 us -> none  [the longest x1 21.1 us: attend_back(): lax.scan(one_block, (zeros_pad, zeros_pad), (offsets, log_norm))]
  transfers between devices with their start and end apart: 14 -> 4, of which waited for: 11 -> 2; matrix products, arithmetic and copies ran while one was open for 23% -> 6% of each run, Pallas kernels for 0% -> 0%
where the time goes in v1:
time: 601 us; the launch traced here: 593 us
  waiting for transfers between devices  208 us (35%)
  local copies, waits for them, and re-layouts  201 us (33%)
  blocking collectives  62.5 us (10%)
  matrix products  40.8 us (7%)
  other arithmetic  37.4 us (6%)
  Pallas kernels  24.4 us (4%)
  between operations  15.6 us (3%)
    reduce_scatter x1, waiting for transfers between devices, shards(): lax.psum_scatter(grads, ('batch', 'mp'), scatter_dimension=0, tiled=False)  136 us
    concatenate x6, local copies, waits for them, and re-layouts, shards(): jnp.concatenate([grad_w_qkv.astype(BF16).reshape(width, 3, n_mp, part).tr...  83.7 us
    all_gather x1, waiting for transfers between devices, shards(): full = lax.all_gather(packed, ('batch', 'mp'), axis=0, tiled=False)  71.9 us
    unnamed x1, blocking collectives  45.5 us
    transpose x1, local copies, waits for them, and re-layouts, shards(): grads.reshape(n_batch, shard, n_mp, -1).transpose(0, 2, 1, 3)  27.8 us
    unnamed x112, local copies, waits for them, and re-layouts  19.6 us
    all_gather x1, blocking collectives, shards(): lax.all_gather(dconv_kernel, 'mp', axis=2, tiled=True).transpose(1, 0, 2)  17.1 us
    dot_general x4, matrix products, tn(): lax.dot_general(left, right, (((0,), (0,)), ((), ())), preferred_element_...  15.4 us
  transfers between devices with their start and end apart: 4, of which 2 were waited for; matrix products, arithmetic and copies ran while one was open for 6% of the time, Pallas kernels for 0%

profile of v1, /device:TPU:0, one launch (start us, length us, event | category | flops | bytes accessed | tf_op | source)
XLA Modules:
  0.0 593.0 jit_solution(5937670839137561003)
XLA Ops:
  9.4 1.9 concatenate.56
  12.3 2.4 collective-permute-start
  17.4 17.1 %all_gather.9 = f32[3,3,768]{1,0,2:T(4,128)S(1)} all-gather(f32[3,3,192]{1,0,2:T(4,128)S(1)} %copy.76), channel_id=1, replica_groups=mesh['mp'=4,'batch'=8] {'mp'}, dimensions={2}, use_global_device_ids=true | all-gather | bytes 34560 | tf_op jit(solution)/shard_map/all_gather | solution.py:180
  34.5 3.5 fusion.15
  38.0 1.9 copy.77
  39.9 1.7 copy.85
  47.2 71.9 %all-gather.3.cloned.1.call-done = bf16[3072,2304]{1,0:T(8,128)(2,1)} async-done(((bf16[96,2304]{1,0:T(8,128)(2,1)}), bf16[3072,2304]{1,0:T(8,128)(2,1)}) %all-gather.3.cloned.1.call-update) | async-done | bytes 14155792 | tf_op jit(solution)/shard_map/all_gather | solution.py:173
  119.1 6.8 %copy.81 = bf16[8,96,4,2304]{3,1,0,2:T(8,128)(2,1)S(1)} copy(bf16[8,96,4,2304]{3,1,2,0:T(8,128)(2,1)} %bitcast.68) | data formatting | bytes 28311552 | tf_op jit(solution)/shard_map/transpose | solution.py:174
  125.9 2.4 slice.148
  128.3 3.1 copy-done.1
  131.4 2.2 slice.140
  133.6 8.1 %fusion.13 = (bf16[768,4,768]{2,0,1:T(8,128)(2,1)}, bf16[768,4,768]{2,0,1:T(8,128)(2,1)}) fusion(bf16[768,4,2304]{2,0,1:T(8,128)(2,1)} %bitcast.64), kind=kLoop, calls=%fused_computation.65 | loop fusion | bytes 18874368 | tf_op jit(solution)/shard_map/slice | solution.py:178
  141.7 4.4 copy.82
  147.5 3.1 fusion.2
  150.7 5.1 add_convert_fusion.1
  160.4 6.7 %copy.88 = bf16[768,4,768]{0,2,1:T(8,128)(2,1)} copy(bf16[768,4,768]{2,0,1:T(8,128)(2,1)} %get-tuple-element.72) | data formatting | bytes 9437184 | tf_op jit(solution)/shard_map/slice | solution.py:178
  167.1 6.7 %copy.89 = bf16[768,4,768]{0,2,1:T(8,128)(2,1)} copy(bf16[768,4,768]{2,0,1:T(8,128)(2,1)} %get-tuple-element.73) | data formatting | bytes 9437184 | tf_op jit(solution)/shard_map/slice | solution.py:179
  173.8 11.9 %attend.1 = (bf16[512,768]{1,0:T(8,128)(2,1)}, bf16[6,2,2,512,256]{4,3,2,1,0:T(8,128)(2,1)}) custom-call(bf16[512,768]{1,0:T(8,128)(2,1)} %slice.145.q_ref, bf16[768,768]{1,0:T(8,128)(2,1)} %get-tuple-element.78.k_ref, bf16[768,768]{1,0:T(8,128)(2,1)} %get-tuple-element.77.v_ref, s32[768,1]{1,0:T(8,128)} %broadcast_in_dim.6.seg_key_ref, s32[1,512]{1,0:T(1,128)} %bitcast.88), custom_call_target="tpu_custom_call" | custom-call | tf_op jit(solution)/shard_map/attend/pallas_call | solution.py:90
  185.8 2.5 multiply_reduce_fusion.8
  188.7 2.7 fusion.12
  191.4 4.5 convolution_convert_fusion.1
  195.9 2.9 multiply_convert_fusion
  198.8 3.3 multiply_reduce_fusion.4
  202.1 4.5 convolution_convert_fusion.2
  207.9 1.7 convolution_convert_fusion.4.grad_ref
  210.6 9.7 %concatenate.72 = bf16[8,96,4,768]{3,2,1,0:T(4,128)(2,1)} reshape(bf16[768,3072]{1,0:T(8,128)(2,1)} %convolution_convert_fusion.1) | data formatting | bytes 9437184 | tf_op jit(solution)/shard_map/concatenate | solution.py:254
  220.3 10.1 %concatenate.71 = bf16[8,96,4,768]{3,2,1,0:T(4,128)(2,1)} reshape(bf16[768,3072]{1,0:T(8,128)(2,1)} %convolution_convert_fusion.2) | data formatting | bytes 9437184 | tf_op jit(solution)/shard_map/concatenate | solution.py:254
  230.4 2.3 concatenate.70
  232.7 12.5 %attend_back.1 = (f32[512,768]{1,0:T(8,128)}, f32[768,768]{1,0:T(8,128)}, f32[768,768]{1,0:T(8,128)}) custom-call(bf16[512,768]{1,0:T(8,128)(2,1)} %slice.145.q_ref, bf16[768,768]{1,0:T(8,128)(2,1)} %get-tuple-element.78.k_ref, bf16[768,768]{1,0:T(8,128)(2,1)} %get-tuple-element.77.v_ref, bf16[512,768]{1,0:T(8,128)(2,1)} %convolution_convert_fusion.4.grad_ref, ...), custom_call_target="tpu_custom_call" | custom-call | tf_op jit(solution)/shard_map/attend_back/pallas_call | solution.py:118
  245.2 14.1 %multiply_reduce_fusion.1 = (f32[2304]{0:T(1024)}, f32[784,2304]{1,0:T(8,128)S(1)}, f32[2304]{0:T(1024)}, f32[2304]{0:T(1024)}, f32[784,2304]{1,0:T(8,128)S(1)}) fusion(f32[783,2304]{1,0:T(8,128)} %bitcast.60, f32[784]{0:T(1024)S(1)} %get-tuple-element.86, f32[768,768]{1,0:T(8,128)} %get-tuple-element.18, f32[768,768]{1,0:T(8,128)} %get-tuple-element.17, ...), kind=kLoop, calls=%fused_computation.7 | loop fusion | flops 32507136 | bytes 42424448 | tf_op jit(solution)/shard_map/reduce_sum | solution.py:238
  259.3 3.3 slice.151
  262.6 4.1 slice.152
  270.0 4.9 add_convert_fusion
  274.9 1.8 copy-done.24
  276.7 5.5 convolution_convert_fusion
  282.2 4.5 copy.91
  286.7 8.1 %copy.98 = bf16[768,4,3,192]{3,2,1,0:T(4,128)(2,1)} copy(bf16[768,4,3,192]{0,3,1,2:T(8,128)(2,1)S(1)} %bitcast.69) | data formatting | bytes 7077888 | tf_op jit(solution)/shard_map/concatenate | solution.py:254
  294.9 14.0 %reshape.161 = bf16[8,96,4,576]{3,2,1,0:T(4,128)(2,1)} reshape(bf16[768,4,3,192]{3,2,1,0:T(4,128)(2,1)} %copy.98) | data formatting | bytes 7077888 | tf_op jit(solution)/shard_map/concatenate | solution.py:254
  308.9 39.4 %concatenate.73 = bf16[8,96,4,2304]{3,2,1,0:T(4,128)(2,1)} concatenate(bf16[8,96,4,576]{3,2,1,0:T(4,128)(2,1)} %reshape.161, bf16[8,96,4,192]{3,2,1,0:T(4,128)(2,1)S(1)} %copy-done.13, bf16[8,96,4,768]{3,2,1,0:T(4,128)(2,1)} %concatenate.71, bf16[8,96,4,768]{3,2,1,0:T(4,128)(2,1)} %concatenate.72), dimensions={3} | concatenate | bytes 28311552 | tf_op jit(solution)/shard_map/concatenate | solution.py:254
  348.3 27.8 %copy.94 = bf16[8,4,96,2304]{2,3,1,0:T(8,128)(2,1)} copy(bf16[8,4,96,2304]{3,1,2,0:T(4,128)(2,1)} %bitcast.65) | data formatting | bytes 28311552 | tf_op jit(solution)/shard_map/transpose | solution.py:263
  376.2 2.1 copy-done.8
  378.4 1.8 broadcast_multiply_fusion.2
  380.2 5.7 fusion.16
  388.9 3.5 add_convert_fusion.2
  392.8 2.7 multiply_reduce_fusion.5
  395.7 45.5 %all-reduce.10 = f32[32,11,24]{2,0,1:T(8,128)S(1)} all-reduce(f32[32,11,24]{2,0,1:T(8,128)S(1)} %maximum_bitcast_fusion), channel_id=3, replica_groups=mesh['mp'=4,'batch'=8] {'mp','batch'}, use_global_device_ids=true, to_apply=%region_9.10.clone | all-reduce | flops 8448 | bytes 67584
  442.3 3.4 multiply_add_fusion
  445.7 135.8 %reduce-scatter.3.cloned.1.call-done = bf16[1,96,2304]{1,2,0:T(8,128)(2,1)} async-done(((bf16[32,96,2304]{1,2,0:T(8,128)(2,1)}), bf16[1,96,2304]{1,2,0:T(8,128)(2,1)}) %reduce-scatter.3.cloned.1.call-update) | async-done | bytes 442384 | tf_op jit(solution)/shard_map/reduce_scatter | solution.py:264
  (161 shorter events, 31.8 us)
Async XLA Ops:
  7.2 7.6 %copy-start.35 = (s32[2048]{0:T(1024)S(1)}, s32[2048]{0:T(1024)}, u32[]{:S(2)}) copy-start(s32[2048]{0:T(1024)} %param.12) | copy-start | bytes 24580
  7.2 10.0 %copy-start.43 = (f32[3,3,192]{2,1,0:T(4,128)S(1)}, f32[3,3,192]{2,1,0:T(4,128)}, u32[]{:S(2)}) copy-start(f32[3,3,192]{2,1,0:T(4,128)} %param.17) | copy-start | bytes 20740
  7.2 111.9 %all-gather.3.cloned.1.call-start = ((), (), s32[]{:S(2)}) async-start(), calls=%async_computation.2 | async-start | bytes 14598144 | tf_op jit(solution)/shard_map/all_gather | solution.py:173
  11.2 570.3 %reduce-scatter.3.cloned.1.call-start = ((), (), s32[]{:S(2)}) async-start(), calls=%async_computation.1 | async-start | bytes 19464192 | tf_op jit(solution)/shard_map/reduce_scatter | solution.py:264
  12.3 32.4 %collective-permute-start = (bf16[272,768]{1,0:T(8,128)(2,1)S(1)}, bf16[272,768]{1,0:T(8,128)(2,1)S(1)}, u32[]{:S(2)}, u32[]{:S(2)}) collective-permute-start(bf16[272,768]{1,0:T(8,128)(2,1)S(1)} %slice.107), channel_id=1, source_target_pairs={{0,8},{8,16},{16,24},{1,9},{9,17},{17,25},{2,10},{10,18},{18,26},{... | collective-permute-start | bytes 1253384 | tf_op jit(solution)/shard_map/ppermute | solution.py:183
  38.0 6.7 %copy-start.5 = (bf16[512,768]{1,0:T(8,128)(2,1)S(1)}, bf16[512,768]{1,0:T(8,128)(2,1)}, u32[]{:S(2)}) copy-start(bf16[512,768]{1,0:T(8,128)(2,1)} %param.11) | copy-start | bytes 2359300
  44.7 1.9 copy-start.20
  125.9 5.5 copy-start.1
  146.4 4.2 copy-start.26
  147.5 3.2 copy-start.29
  147.5 3.2 copy-start.30
  147.5 3.2 copy-start.34
  150.7 5.2 copy-start
  156.8 2.2 copy-start.14
  173.8 12.0 %copy-start.11 = (f32[784,768]{1,0:T(8,128)S(1)}, f32[784,768]{1,0:T(8,128)}, u32[]{:S(2)}) copy-start(f32[784,768]{1,0:T(8,128)} %maximum_convert_fusion) | copy-start | bytes 7225348
  173.8 12.0 %copy-start.38 = (f32[512]{0:T(512)S(1)}, f32[512]{0:T(512)}, u32[]{:S(2)}) copy-start(f32[512]{0:T(512)} %fusion.7) | copy-start | bytes 6148
  185.8 2.9 copy-start.18
  185.8 2.9 copy-start.45
  188.3 18.3 %copy-start.15 = (f32[512,768]{1,0:T(8,128)}, f32[512,768]{1,0:T(8,128)S(1)}, u32[]{:S(2)}) copy-start(f32[512,768]{1,0:T(8,128)S(1)} %get-tuple-element.89) | copy-start | bytes 4718596
  188.7 2.7 copy-start.28
  188.7 7.2 %slice-start = ((s8[4718592]{0:T(1024)(128)(4,1)}), s8[4194304]{0:T(1024)(128)(4,1)S(1)}, s32[]{:S(2)}) async-start(s8[4718592]{0:T(1024)(128)(4,1)} %bitcast.70), calls=%async_computation.3 | async-start | bytes 8388608
  191.4 4.5 copy-start.46
  191.4 4.5 slice-start.1
  262.6 5.7 copy-start.2
  262.6 6.3 %copy-start.9 = (f32[768,768]{1,0:T(8,128)S(1)}, f32[768,768]{1,0:T(8,128)}, u32[]{:S(2)}) copy-start(f32[768,768]{1,0:T(8,128)} %get-tuple-element.17) | copy-start | bytes 7077892
  262.6 7.0 %copy-start.10 = (f32[768,768]{1,0:T(8,128)S(1)}, f32[768,768]{1,0:T(8,128)}, u32[]{:S(2)}) copy-start(f32[768,768]{1,0:T(8,128)} %get-tuple-element.18) | copy-start | bytes 7077892
  262.6 7.4 %copy-start.12 = (f32[512,768]{1,0:T(8,128)S(1)}, f32[512,768]{1,0:T(8,128)}, u32[]{:S(2)}) copy-start(f32[512,768]{1,0:T(8,128)} %get-tuple-element.16) | copy-start | bytes 4718596
  270.0 6.7 %copy-start.7 = (bf16[512,768]{1,0:T(8,128)(2,1)S(1)}, bf16[512,768]{1,0:T(8,128)(2,1)}, u32[]{:S(2)}) copy-start(bf16[512,768]{1,0:T(8,128)(2,1)} %param.11) | copy-start | bytes 2359300
  270.0 6.7 %copy-start.22 = (bf16[272,768]{1,0:T(8,128)(2,1)S(1)}, bf16[272,768]{1,0:T(8,128)(2,1)}, u32[]{:S(2)}) copy-start(bf16[272,768]{1,0:T(8,128)(2,1)} %copy-done.20) | copy-start | bytes 1253380
  270.0 6.7 %copy-start.37 = (f32[784]{0:T(1024)S(1)}, f32[784]{0:T(1024)}, u32[]{:S(2)}) copy-start(f32[784]{0:T(1024)} %add_rsqrt_fusion) | copy-start | bytes 9412
  270.0 6.7 %copy-start.41 = (f32[768]{0:T(1024)S(1)}, f32[768]{0:T(1024)}, u32[]{:S(2)}) copy-start(f32[768]{0:T(1024)} %param.14) | copy-start | bytes 9220
  294.9 14.0 %copy-start.13 = (bf16[8,96,4,192]{3,2,1,0:T(4,128)(2,1)S(1)}, bf16[8,96,4,192]{3,2,1,0:T(4,128)(2,1)}, u32[]{:S(2)}) copy-start(bf16[8,96,4,192]{3,2,1,0:T(4,128)(2,1)} %concatenate.70) | copy-start | bytes 3538948
  376.1 2.2 copy-start.8
  376.1 2.3 copy-start.23
  376.1 12.7 %slice-start.2 = ((s8[4718592]{0:T(1024)(128)(4,1)}), s8[524288]{0:T(1024)(128)(4,1)S(1)}, s32[]{:S(2)}) async-start(s8[4718592]{0:T(1024)(128)(4,1)} %bitcast.73), calls=%async_computation.5 | async-start | bytes 1048576
  376.1 4.1 copy-start.25
  378.4 10.4 %slice-start.4 = ((s8[6291456]{0:T(1024)(128)(4,1)}), s8[4194304]{0:T(1024)(128)(4,1)S(1)}, s32[]{:S(2)}) async-start(s8[6291456]{0:T(1024)(128)(4,1)} %bitcast.89), calls=%async_computation.7 | async-start | bytes 8388608
  380.2 8.7 %copy-start.16 = (f32[512,768]{1,0:T(8,128)S(1)}, f32[512,768]{1,0:T(8,128)}, u32[]{:S(2)}) copy-start(f32[512,768]{1,0:T(8,128)} %copy-done.15) | copy-start | bytes 4718596
  380.2 8.7 %slice-start.3 = ((s8[4718592]{0:T(1024)(128)(4,1)}), s8[4194304]{0:T(1024)(128)(4,1)S(1)}, s32[]{:S(2)}) async-start(s8[4718592]{0:T(1024)(128)(4,1)} %bitcast.73), calls=%async_computation.6 | async-start | bytes 8388608
  380.2 8.7 %copy-start.39 = (f32[512]{0:T(512)S(1)}, f32[512]{0:T(512)}, u32[]{:S(2)}) copy-start(f32[512]{0:T(512)} %fusion.7) | copy-start | bytes 6148
  380.2 8.7 %slice-start.5 = ((s8[6291456]{0:T(1024)(128)(4,1)}), s8[2097152]{0:T(1024)(128)(4,1)S(1)}, s32[]{:S(2)}) async-start(s8[6291456]{0:T(1024)(128)(4,1)} %bitcast.89), calls=%async_computation.8 | async-start | bytes 4194304
  387.4 5.1 copy-start.44
  387.4 5.2 copy-start.33
  387.4 5.2 copy-start.32
  387.4 5.2 copy-start.31
  387.4 5.4 copy-start.42
  387.4 5.4 collective-permute-start.1
  392.4 49.8 %copy-start.4 = (f32[512,768]{1,0:T(8,128)S(1)}, f32[512,768]{1,0:T(8,128)}, u32[]{:S(2)}) copy-start(f32[512,768]{1,0:T(8,128)} %copy-done.3) | copy-start | bytes 4718596
  (9 other events, 13.1 us)
Sparse Core Ops, SparseCore 0:
  11.5 107.5 all-gather.2
  376.3 205.2 reduce-scatter.2

commit v2 on v1

--- a/solution.py
+++ b/solution.py
@@ -156,7 +156,7 @@
     return jnp.concatenate([values[by:], jnp.zeros((by,) + values.shape[1:], values.dtype)], axis=0)
 
 
-def shards(
+def shards_plain(
     tokens, seg_ids, counts, gain_attn, gain_ffn, w_qkv, dconv_kernel, w_out, w_up, w_down, grad_out
 ):
     rows, width = tokens.shape
@@ -281,6 +281,355 @@
     )
 
 
+HALO = SEQ_MAX
+BLK = 128
+HEADS = ((1, 2, 3, False, False, 0), (1, 2, 3, True, True, 0), (0, 4, 4, True, False, 1))
+COLUMNS = 5 * BLK
+
+
+def blk(index):
+    return slice(index * BLK, (index + 1) * BLK)
+
+
+def half_of(values, upper):
+    lane = lax.broadcasted_iota(jnp.int32, values.shape, 1)
+    keep = (lane >= HD) if upper else (lane < HD)
+    return jnp.where(keep, values, jnp.zeros_like(values))
+
+
+def rows_loop(total, size, body):
+    def one(i, carry):
+        body(pl.ds(pl.multiple_of(i * size, size), size))
+        return carry
+
+    lax.fori_loop(0, total // size, one, 0)
+
+
+def parts_loop(count, body):
+    def one(i, carry):
+        body(i)
+        return carry
+
+    lax.fori_loop(0, count, one, 0)
+
+
+def layer_kernel(
+    wa_hbm, wu_hbm, wd_hbm, ext_ref, grad_ref, cols_ref, seg_row_ref, gains_ref, kernel_ref,
+    ga_hbm, gu_hbm, gd_hbm, out_ref, resid_grad_ref, own_ref, pass_ref, small_ref, gain_ref,
+    wa, wu, wd, ga, gu, gd, normed, proj, mixed, prob, heads, bias, wide, acc, resid, normed_two,
+    gffn_t, two_t, normed_t, hidden, upper, lower, in_sems, out_sems,
+):
+    parts = wa.shape[0]
+    rows, width = resid.shape
+    span = HALO + rows
+    tiles = rows // SEQ_MAX
+    tile = SEQ_MAX
+
+    def fetch(hbm, ref, piece, m):
+        return pltpu.make_async_copy(hbm.at[m], ref.at[m], in_sems.at[piece, m])
+
+    def put(ref, hbm, piece, m):
+        return pltpu.make_async_copy(ref.at[m], hbm.at[m], out_sems.at[piece, m])
+
+    for m in range(parts):
+        fetch(wa_hbm, wa, 0, m).start()
+    for m in range(parts):
+        fetch(wu_hbm, wu, 1, m).start()
+        fetch(wd_hbm, wd, 2, m).start()
+
+    gain_one = gains_ref[0:1, :]
+    gain_two = gains_ref[1:2, :]
+
+    def norm_one(at):
+        values = ext_ref[at, :].astype(F32)
+        normed[at, :] = (values * rms(values) * gain_one).astype(BF16)
+
+    rows_loop(span, 128, norm_one)
+    for at in range(tiles):
+        key = lax.broadcasted_iota(jnp.int32, (2 * tile, tile), 0)
+        query = lax.broadcasted_iota(jnp.int32, (2 * tile, tile), 1) + tile
+        seg_key = cols_ref[at * tile : (at + 2) * tile, 2:3]
+        same = seg_key == seg_row_ref[0:1, at * tile : (at + 1) * tile]
+        bias[at] = jnp.where(same & (key <= query), 0.0, MASKED).astype(F32)
+    acc[...] = jnp.zeros_like(acc)
+
+    def forward(m):
+        fetch(wa_hbm, wa, 0, m).wait()
+        wide[...] = nn(normed[...], wa[m, :, BLK:])
+        for c in range(5):
+            source = wide[:, blk(c)]
+            proj[m, :, blk(c)] = source.astype(BF16)
+            mixed[m, :, blk(c)] = (
+                kernel_ref[m, 0:1, blk(c)] * source
+                + kernel_ref[m, 1:2, blk(c)] * (cols_ref[:, 0:1] * pltpu.roll(source, 1, 0))
+                + kernel_ref[m, 2:3, blk(c)] * (cols_ref[:, 1:2] * pltpu.roll(source, 2, 0))
+            ).astype(BF16)
+        for at in range(tiles):
+            keys_at = slice(at * tile, (at + 2) * tile)
+            query_at = slice(HALO + at * tile, HALO + (at + 1) * tile)
+            outs = []
+            for h, (qb, kb, vb, qk_upper, v_upper, _) in enumerate(HEADS):
+                queries = half_of(mixed[m, query_at, blk(qb)], qk_upper) * jnp.asarray(HD**-0.5, BF16)
+                scores = nt(mixed[m, keys_at, blk(kb)], queries) + bias[at]
+                expo = jnp.exp(scores - jnp.max(scores, axis=0, keepdims=True))
+                share = (expo * (1.0 / jnp.sum(expo, axis=0, keepdims=True))).astype(BF16)
+                prob[m, at, h] = share
+                outs.append(tn(half_of(mixed[m, keys_at, blk(vb)], v_upper), share))
+            own_at = slice(at * tile, (at + 1) * tile)
+            heads[m, own_at, blk(0)] = (outs[0] + outs[1]).T.astype(BF16)
+            heads[m, own_at, blk(1)] = outs[2].T.astype(BF16)
+        acc[...] += nt(heads[m], wa[m, :, : 2 * BLK])
+
+    parts_loop(parts, forward)
+
+    def middle(at):
+        values = ext_ref[pl.ds(at.start + HALO, at.size), :].astype(F32)
+        filled = cols_ref[pl.ds(at.start + HALO, at.size), 3:4]
+        value = values + filled * acc[at, :]
+        resid[at, :] = value
+        normed_two[at, :] = (value * rms(value) * gain_two).astype(BF16)
+        out_ref[at, :] = (filled * grad_ref[at, :].astype(F32)).astype(BF16)
+
+    rows_loop(rows, 128, middle)
+    gffn = out_ref
+    gffn_t[...] = gffn[...].T
+    two_t[...] = normed_two[...].T
+    normed_t[...] = normed[...].T
+    acc[...] = jnp.zeros_like(acc)
+    own_ref[...] = jnp.zeros_like(own_ref)
+
+    def feed(m):
+        fetch(wu_hbm, wu, 1, m).wait()
+        fetch(wd_hbm, wd, 2, m).wait()
+        up = jnp.maximum(nn(normed_two[...], wu[m]), 0.0)
+        upper[...] = (2.0 * up).astype(BF16)
+        hidden[...] = (up * up).astype(BF16)
+        acc[...] += nt(hidden[...], wd[m])
+        gd[m] = nn(gffn_t[...], hidden[...]).astype(BF16)
+        put(gd, gd_hbm, 2, m).start()
+        lower[...] = (nn(gffn[...], wd[m]) * upper[...].astype(F32)).astype(BF16)
+        gu[m] = nn(two_t[...], lower[...]).astype(BF16)
+        put(gu, gu_hbm, 1, m).start()
+        own_ref[...] += nt(lower[...], wu[m])
+
+    parts_loop(parts, feed)
+
+    gain_ref[...] = jnp.zeros_like(gain_ref)
+
+    def turn(at):
+        value = resid[at, :]
+        filled = cols_ref[pl.ds(at.start + HALO, at.size), 3:4]
+        scale = rms(value)
+        hat = value * scale
+        grad = own_ref[at, :]
+        gain_ref[0:1, :] += jnp.sum(grad * hat, axis=0, keepdims=True)
+        total = grad_ref[at, :].astype(F32) + rms_back(grad, gain_two, hat, scale)
+        resid_grad_ref[at, :] = total
+        out_ref[at, :] = (value + filled * acc[at, :]).astype(BF16)
+        normed_two[at, :] = (filled * total).astype(BF16)
+
+    rows_loop(rows, 128, turn)
+    gattn = normed_two
+    two_t[...] = gattn[...].T
+    own_ref[...] = jnp.zeros_like(own_ref)
+    acc[...] = jnp.zeros_like(acc)
+
+    def backward(m):
+        grads = nn(gattn[...], wa[m, :, : 2 * BLK]).astype(BF16)
+        hidden[:, : 2 * BLK] = grads
+        wide[...] = jnp.zeros_like(wide)
+        for at in range(tiles):
+            keys_at = slice(at * tile, (at + 2) * tile)
+            query_at = slice(HALO + at * tile, HALO + (at + 1) * tile)
+            own_at = slice(at * tile, (at + 1) * tile)
+            for h, (qb, kb, vb, qk_upper, v_upper, ob) in enumerate(HEADS):
+                share = prob[m, at, h]
+                grad_head = half_of(hidden[own_at, blk(ob)], v_upper)
+                queries = half_of(mixed[m, query_at, blk(qb)], qk_upper) * jnp.asarray(HD**-0.5, BF16)
+                grad_prob = nt(mixed[m, keys_at, blk(vb)], grad_head)
+                broad = share.astype(F32)
+                inner = broad * grad_prob
+                grad_scores = (inner - broad * jnp.sum(inner, axis=0, keepdims=True)).astype(BF16)
+                wide[keys_at, blk(vb)] += nn(share, grad_head)
+                wide[keys_at, blk(kb)] += nn(grad_scores, queries)
+                keys = half_of(mixed[m, keys_at, blk(kb)], qk_upper)
+                wide[query_at, blk(qb)] += (tn(keys, grad_scores) * HD**-0.5).T
+        for c in range(5):
+            grad = wide[:, blk(c)]
+            one = grad * cols_ref[:, 0:1]
+            two = grad * cols_ref[:, 1:2]
+            source = proj[m, :, blk(c)].astype(F32)
+            small_ref[m, 0:1, blk(c)] = jnp.sum(grad * source, axis=0, keepdims=True)
+            small_ref[m, 1:2, blk(c)] = jnp.sum(one * pltpu.roll(source, 1, 0), axis=0, keepdims=True)
+            small_ref[m, 2:3, blk(c)] = jnp.sum(two * pltpu.roll(source, 2, 0), axis=0, keepdims=True)
+            mixed[m, :, blk(c)] = (
+                kernel_ref[m, 0:1, blk(c)] * grad
+                + kernel_ref[m, 1:2, blk(c)] * pltpu.roll(one, span - 1, 0)
+                + kernel_ref[m, 2:3, blk(c)] * pltpu.roll(two, span - 2, 0)
+            ).astype(BF16)
+        part = nn(two_t[...], heads[m])
+        whole = nn(normed_t[...], mixed[m])
+        ga[m, :, blk(0)] = part[:, blk(0)].astype(BF16)
+        ga[m, :, blk(1)] = (half_of(part[:, blk(1)], False) + half_of(whole[:, blk(0)], True)).astype(BF16)
+        ga[m, :, 2 * BLK :] = whole[:, BLK:].astype(BF16)
+        put(ga, ga_hbm, 0, m).start()
+        own_ref[...] += nt(mixed[m, HALO:, :], wa[m, :, BLK:])
+        acc[:HALO, :] += nt(mixed[m, :HALO, :], wa[m, :, BLK:])
+
+    parts_loop(parts, backward)
+    pass_ref[...] = acc[:HALO, :].astype(BF16)
+    for m in range(parts):
+        put(ga, ga_hbm, 0, m).wait()
+        put(gu, gu_hbm, 1, m).wait()
+        put(gd, gd_hbm, 2, m).wait()
+
+
+def layer_call(wa, wu, wd, ext, grad_out, cols, seg_row, gains, kernel):
+    parts, width, _ = wa.shape
+    rows = grad_out.shape[0]
+    span = rows + HALO
+    tiles = rows // SEQ_MAX
+    vmem = pl.BlockSpec(memory_space=pltpu.VMEM)
+    hbm = pl.BlockSpec(memory_space=pl.ANY)
+    big = pltpu.VMEM((parts, width, width), BF16)
+    return pl.pallas_call(
+        layer_kernel,
+        in_specs=[hbm] * 3 + [vmem] * 6,
+        out_specs=[hbm] * 3 + [vmem] * 6,
+        out_shape=[jax.ShapeDtypeStruct((parts, width, width), BF16)] * 3
+        + [
+            jax.ShapeDtypeStruct((rows, width), BF16),
+            jax.ShapeDtypeStruct((rows, width), F32),
+            jax.ShapeDtypeStruct((rows, width), F32),
+            jax.ShapeDtypeStruct((HALO, width), BF16),
+            jax.ShapeDtypeStruct((parts, 3, COLUMNS), F32),
+            jax.ShapeDtypeStruct((1, width), F32),
+        ],
+        scratch_shapes=[
+            big, big, big, big, big, big,
+            pltpu.VMEM((span, width), BF16),
+            pltpu.VMEM((parts, span, COLUMNS), BF16),
+            pltpu.VMEM((parts, span, COLUMNS), BF16),
+            pltpu.VMEM((parts, tiles, 3, 2 * SEQ_MAX, SEQ_MAX), BF16),
+            pltpu.VMEM((parts, rows, 2 * BLK), BF16),
+            pltpu.VMEM((tiles, 2 * SEQ_MAX, SEQ_MAX), F32),
+            pltpu.VMEM((span, COLUMNS), F32),
+            pltpu.VMEM((rows, width), F32),
+            pltpu.VMEM((rows, width), F32),
+            pltpu.VMEM((rows, width), BF16),
+            pltpu.VMEM((width, rows), BF16),
+            pltpu.VMEM((width, rows), BF16),
+            pltpu.VMEM((width, span), BF16),
+            pltpu.VMEM((rows, width), BF16),
+            pltpu.VMEM((rows, width), BF16),
+            pltpu.VMEM((rows, width), BF16),
+            pltpu.SemaphoreType.DMA((3, parts)),
+            pltpu.SemaphoreType.DMA((3, parts)),
+        ],
+        compiler_params=pltpu.CompilerParams(vmem_limit_bytes=67043328),
+        name="layer",
+    )(wa, wu, wd, ext, grad_out, cols, seg_row, gains, kernel)
+
+
+def arrange(q, k, v, o):
+    cut = lambda a, h: a[..., h * HD : (h + 1) * HD]
+    order = [cut(o, 0), cut(o, 1), cut(o, 2), cut(q, 2), cut(q, 0), cut(q, 1)]
+    order += [cut(k, 0), cut(k, 1), cut(v, 0), cut(v, 1), cut(v, 2), cut(k, 2)]
+    return jnp.concatenate(order, axis=-1)
+
+
+def disarrange(a):
+    cut = lambda i: a[..., i * HD : (i + 1) * HD]
+    join = lambda *ids: jnp.concatenate([cut(i) for i in ids], axis=-1)
+    return join(4, 5, 3), join(6, 7, 11), join(8, 9, 10), join(0, 1, 2)
+
+
+def shards(
+    tokens, seg_ids, counts, gain_attn, gain_ffn, w_qkv, dconv_kernel, w_out, w_up, w_down, grad_out
+):
+    rows, width = tokens.shape
+    n_mp = lax.axis_size("mp")
+    n_batch = lax.axis_size("batch")
+    part = width // n_mp
+    shard = w_qkv.shape[0]
+    fits = (
+        rows % SEQ_MAX == 0 and part == 3 * HD and width == 4 * part and shard % 16 == 0
+        and w_up.shape[1] == width and seg_ids.shape[0] == n_mp * rows
+    )
+    if not fits:
+        return shards_plain(
+            tokens, seg_ids, counts, gain_attn, gain_ffn, w_qkv, dconv_kernel, w_out, w_up, w_down, grad_out
+        )
+    own_start = lax.axis_index("mp") * rows
+    piece_a = arrange(w_qkv[:, 0], w_qkv[:, 1], w_qkv[:, 2], w_out.T)
+    pieces = jnp.stack([piece_a, w_up, w_down.T])
+    wa, wu, wd = gather(pieces)
+    taps = lax.all_gather(dconv_kernel, "mp", axis=0, tiled=False)
+    zero = jnp.zeros_like(taps[:, 0])
+    kernel = arrange(taps[:, 0], taps[:, 1], taps[:, 2], zero)[..., BLK:]
+    back = [(i, i + 1) for i in range(n_mp - 1)]
+    ext = jnp.concatenate([lax.ppermute(tokens[rows - HALO :], "mp", back), tokens], axis=0)
+    seg_pad = jnp.concatenate([jnp.full((HALO,), -1, jnp.int32), seg_ids])
+    seg = lax.dynamic_slice_in_dim(seg_pad, own_start, HALO + rows, 0).astype(F32)
+    slot = own_start - HALO + lax.iota(jnp.int32, HALO + rows)
+    cols = jnp.stack(
+        [
+            (seg == later(seg, 1)).astype(F32).at[0].set(0.0),
+            (seg == later(seg, 2)).astype(F32).at[:2].set(0.0),
+            seg,
+            (slot < counts[0]).astype(F32),
+        ],
+        axis=1,
+    )
+    gains = jnp.stack([gain_attn, gain_ffn])
+    ga, gu, gd, layer_out, resid_grad, own_normed, passed, taps_grad, gain_two = layer_call(
+        wa, wu, wd, ext, grad_out, cols, seg[None, HALO:], gains, kernel
+    )
+    own = scatter(ga, gu, gd)
+    ahead = [(i + 1, i) for i in range(n_mp - 1)]
+    passed = lax.ppermute(passed, "mp", ahead).astype(F32)
+    own_normed = own_normed + jnp.pad(passed, ((rows - HALO, 0), (0, 0)))
+    values = tokens.astype(F32)
+    scale = rms(values)
+    hat = values * scale
+    grad_tokens = resid_grad + rms_back(own_normed, gain_attn, hat, scale)
+    gain_one = jnp.sum(own_normed * hat, axis=0)
+    first, second, third, _ = disarrange(jnp.pad(taps_grad, ((0, 0), (0, 0), (BLK, 0))))
+    small = jnp.stack([first, second, third]).transpose(0, 2, 1, 3).reshape(9, width)
+    small = jnp.concatenate([small, gain_one[None], gain_two])
+    piece = width // (n_mp * n_batch)
+    small = small.reshape(11, n_mp * n_batch, piece).transpose(1, 0, 2)
+    small = lax.psum_scatter(small, ("mp", "batch"), scatter_dimension=0, tiled=False)
+    q, k, v, o = disarrange(own[0])
+    return (
+        layer_out,
+        grad_tokens,
+        small[9],
+        small[10],
+        jnp.stack([q, k, v], axis=1),
+        small[:9].reshape(3, 3, piece),
+        o.T,
+        own[1],
+        own[2].T,
+    )
+
+
+def gather(pieces):
+    full = lax.all_gather(pieces, ("batch", "mp"), axis=0, tiled=False)
+    n_mp = lax.axis_size("mp")
+    full = full.reshape((-1, n_mp) + pieces.shape).transpose(2, 1, 0, 3, 4)
+    full = full.reshape(3, n_mp, -1, pieces.shape[2])
+    return full[0], full[1], full[2]
+
+
+def scatter(ga, gu, gd):
+    n_mp, width, columns = ga.shape
+    n_batch = lax.axis_size("batch")
+    grads = jnp.stack([ga, gu, gd]).reshape(3, n_mp, n_batch, width // n_batch, columns)
+    grads = grads.transpose(2, 1, 0, 3, 4).reshape((-1, 3, width // n_batch, columns))
+    return lax.psum_scatter(grads, ("batch", "mp"), scatter_dimension=0, tiled=False).astype(F32)
+
+
 def solution(mesh):
     in_specs = (
         P(("batch", "mp"), None),

time: 601 us -> 377 us (0.63); the launches traced: 593 us -> 376 us
  local copies, waits for them, and re-layouts: 201 us -> 26.7 us
  matrix products: 40.8 us -> 0 us
  Pallas kernels: 24.4 us -> 63.2 us
  other arithmetic: 37.4 us -> 16.2 us
  blocking collectives: 62.5 us -> 52.7 us
  waiting for transfers between devices: 208 us -> 199 us
    concatenate x10 -> x5, local copies, waits for them, and re-layouts: 85.8 us -> 1.1 us  [the longest x2 0.82 us: arrange(): return jnp.concatenate(order, axis=-1)]
    slice x21 -> x16, local copies, waits for them, and re-layouts: 51.5 us -> 6.29 us  [the longest x1 5.47 us: gather(): return (full[0], full[1], full[2])]
    dot_general x12 -> x0, matrix products: 40.8 us -> none  [the longest x4 15.4 us: tn(): lax.dot_general(left, right, (((0,), (0,)), ((), ())), preferred_element_...]
    pallas_call x2 -> x1, Pallas kernels: 24.4 us -> 63.2 us  [layer_call(): pl.pallas_call(layer_kernel, in_specs=[hbm] * 3 + [vmem] * 6, out_specs=[...]
    reduce_scatter x1, waiting for transfers between devices: 136 us -> 105 us  [scatter(): lax.psum_scatter(grads, ('batch', 'mp'), scatter_dimension=0, tiled=False)]
    transpose x6 -> x4, local copies, waits for them, and re-layouts: 35.6 us -> 6.52 us  [the longest x1 5.62 us: scatter(): grads.transpose(2, 1, 0, 3, 4).reshape((-1, 3, width // n_batch, columns))]
    all_gather x1, waiting for transfers between devices: 71.9 us -> 91.5 us  [gather(): full = lax.all_gather(pieces, ('batch', 'mp'), axis=0, tiled=False)]
    unnamed x112 -> x24, local copies, waits for them, and re-layouts: 19.6 us -> 2.75 us
  transfers between devices with their start and end apart: 4 -> 4, of which waited for: 2 -> 3; matrix products, arithmetic and copies ran while one was open for 6% -> 3% of each run, Pallas kernels for 0% -> 0%
where the time goes in v2:
time: 377 us; the launch traced here: 376 us
  waiting for transfers between devices  199 us (53%)
  Pallas kernels  63.2 us (17%)
  blocking collectives  52.7 us (14%)
  local copies, waits for them, and re-layouts  26.7 us (7%)
  other arithmetic  16.2 us (4%)
  between operations  15.1 us (4%)
  starting transfers between devices  3.79 us (1%)
    reduce_scatter x1, waiting for transfers between devices, scatter(): lax.psum_scatter(grads, ('batch', 'mp'), scatter_dimension=0, tiled=False)  105 us
    all_gather x1, waiting for transfers between devices, gather(): full = lax.all_gather(pieces, ('batch', 'mp'), axis=0, tiled=False)  91.5 us
    pallas_call x1, Pallas kernels, layer_call(): pl.pallas_call(layer_kernel, in_specs=[hbm] * 3 + [vmem] * 6, out_specs=[...  63.2 us
    unnamed x1, blocking collectives  46.2 us
  transfers between devices with their start and end apart: 4, of which 3 were waited for; matrix products, arithmetic and copies ran while one was open for 3% of the time, Pallas kernels for 0%

profile of v2, /device:TPU:0, one launch (start us, length us, event | category | flops | bytes accessed | tf_op | source)
XLA Modules:
  0.0 376.5 jit_solution(1274739867878503283)
XLA Ops:
  7.2 0.0 copy-start
  7.2 0.0 all-gather.4.cloned.1.call-start
  7.3 0.9 slice_bitcast_fusion.5
  8.2 0.9 copy.36
  9.1 0.0 copy-start.4
  9.1 0.0 copy-start.8
  9.1 0.1 concatenate.56
  9.2 1.8 pad_maximum_fusion.1
  11.0 0.0 all-gather.4.cloned.1.call-update
  11.1 0.0 reduce-scatter.3.cloned.1.call-start
  11.2 2.4 collective-permute-start
  13.6 6.5 %all-gather.1 = f32[12,3,192]{2,1,0:T(4,128)S(1)} all-gather(f32[3,3,192]{2,1,0:T(4,128)S(1)} %copy-done.7), channel_id=3, replica_groups=mesh['mp'=4,'batch'=8] {'mp'}, dimensions={0}, use_global_device_ids=true | all-gather | bytes 34560 | tf_op jit(solution)/shard_map/all_gather | solution.py:567
  20.1 0.1 fusion.9
  20.2 0.1 fusion.11
  20.3 0.6 slice.207
  21.6 0.2 scatter.9
  21.8 1.0 copy.41.cols_ref
  22.8 0.7 concatenate.61.kernel_ref
  23.5 0.6 pad_maximum_fusion.4.gains_ref
  24.1 0.0 collective-permute-done
  24.1 1.1 pad_maximum_fusion.ext_ref
  25.2 91.5 %all-gather.4.cloned.1.call-done = bf16[96,96,768]{2,1,0:T(8,128)(2,1)} async-done(((bf16[3,96,768]{2,1,0:T(8,128)(2,1)}), bf16[96,96,768]{2,1,0:T(8,128)(2,1)}) %all-gather.4.cloned.1.call-update) | async-done | bytes 14155792 | tf_op jit(solution)/shard_map/all_gather | solution.py:618
  116.7 6.8 %copy.52 = bf16[8,4,3,96,768]{4,3,0,1,2:T(8,128)(2,1)S(1)} copy(bf16[8,4,3,96,768]{4,3,2,1,0:T(8,128)(2,1)} %bitcast.78) | data formatting | bytes 28311552 | tf_op jit(solution)/shard_map/reshape | solution.py:620
  123.5 5.5 %fusion.14 = (bf16[1,4,8,96,768]{4,3,2,1,0:T(8,128)(2,1)}, bf16[1,4,8,96,768]{4,3,2,1,0:T(8,128)(2,1)}, bf16[1,4,8,96,768]{4,3,2,1,0:T(8,128)(2,1)}) fusion(bf16[3,4,8,96,768]{4,3,2,1,0:T(8,128)(2,1)S(1)} %bitcast.74), kind=kLoop, calls=%fused_computation.51 | loop fusion | bytes 28311552 | tf_op jit(solution)/shard_map/slice | solution.py:622
  129.0 63.2 %layer.1 = (bf16[4,768,768]{2,1,0:T(8,128)(2,1)}, bf16[4,768,768]{2,1,0:T(8,128)(2,1)}, bf16[4,768,768]{2,1,0:T(8,128)(2,1)}, bf16[512,768]{1,0:T(8,128)(2,1)}, ...) custom-call(bf16[4,768,768]{2,1,0:T(8,128)(2,1)} %bitcast.77, ...), custom_call_target="tpu_custom_call" | custom-call | tf_op jit(solution)/shard_map/layer/pallas_call | solution.py:495
  192.1 6.7 %maximum_bitcast_fusion = bf16[8,4,3,96,768]{4,3,0,1,2:T(8,128)(2,1)S(1)} fusion(bf16[1,4,8,96,768]{4,3,2,1,0:T(8,128)(2,1)} %bitcast.81, bf16[1,4,8,96,768]{4,3,2,1,0:T(8,128)(2,1)} %bitcast.80, bf16[1,4,8,96,768]{4,3,2,1,0:T(8,128)(2,1)} %bitcast.79), kind=kLoop, calls=%fused_computation | loop fusion | flops 14155776 | bytes 28311552 | tf_op jit(solution)/shard_map/transpose | solution.py:629
  198.9 5.6 %copy.43 = bf16[8,4,3,96,768]{4,3,2,1,0:T(8,128)(2,1)} copy(bf16[8,4,3,96,768]{4,3,0,1,2:T(8,128)(2,1)S(1)} %maximum_bitcast_fusion) | data formatting | bytes 28311552 | tf_op jit(solution)/shard_map/transpose | solution.py:629
  204.5 0.0 copy-start.5
  204.5 0.0 reduce-scatter.3.cloned.1.call-update
  204.5 1.1 copy-done.1
  205.6 0.2 fusion.8
  205.9 1.3 collective-permute-start.1
  207.2 0.1 fusion.18
  207.3 0.1 concatenate.64
  207.5 0.1 concatenate.66
  207.6 2.2 collective-permute-done.1
  209.8 0.6 fusion.7
  210.4 0.1 concatenate.65
  210.5 46.2 %all-reduce.3 = f32[32,11,24]{2,0,1:T(8,128)S(1)} all-reduce(f32[32,11,24]{2,0,1:T(8,128)S(1)} %maximum_bitcast_fusion.1), channel_id=4, replica_groups=mesh['mp'=4,'batch'=8] {'mp','batch'}, use_global_device_ids=true, to_apply=%region_3.4.clone | all-reduce | flops 8448 | bytes 67584
  256.8 0.6 reshape.136
  257.4 0.5 fusion.13
  257.9 3.2 fusion.6
  261.1 105.0 %reduce-scatter.3.cloned.1.call-done = bf16[1,3,96,768]{3,2,1,0:T(8,128)(2,1)} async-done(((bf16[32,3,96,768]{3,2,1,0:T(8,128)(2,1)}), bf16[1,3,96,768]{3,2,1,0:T(8,128)(2,1)}) %reduce-scatter.3.cloned.1.call-update) | async-done | bytes 442384 | tf_op jit(solution)/shard_map/reduce_scatter | solution.py:630
  366.1 1.1 convert_element_type.30
  367.2 0.9 slice_bitcast_fusion
  368.0 0.1 fusion.16
  368.1 0.7 copy.44
  368.9 0.7 pad_maximum_fusion.2
  (50 shorter events, 0.4 us)
Async XLA Ops:
  7.2 3.9 %copy-start = (bf16[512,768]{1,0:T(8,128)(2,1)S(1)}, bf16[512,768]{1,0:T(8,128)(2,1)}, u32[]{:S(2)}) copy-start(bf16[512,768]{1,0:T(8,128)(2,1)} %param.15) | copy-start | bytes 2359300
  7.2 6.4 %copy-start.7 = (f32[3,3,192]{2,1,0:T(4,128)S(1)}, f32[3,3,192]{2,1,0:T(4,128)}, u32[]{:S(2)}) copy-start(f32[3,3,192]{2,1,0:T(4,128)} %param.21) | copy-start | bytes 20740
  7.2 12.9 %copy-start.6 = (s32[2048]{0:T(1024)S(1)}, s32[2048]{0:T(1024)}, u32[]{:S(2)}) copy-start(s32[2048]{0:T(1024)} %param.16) | copy-start | bytes 24580
  7.2 109.5 %all-gather.4.cloned.1.call-start = ((), (), s32[]{:S(2)}) async-start(), calls=%async_computation.2 | async-start | bytes 14598144 | tf_op jit(solution)/shard_map/all_gather | solution.py:618
  9.1 13.7 %copy-start.4 = (f32[768]{0:T(1024)S(1)}, f32[768]{0:T(1024)}, u32[]{:S(2)}) copy-start(f32[768]{0:T(1024)} %param.18) | copy-start | bytes 9220
  9.1 13.6 %copy-start.8 = (f32[768]{0:T(1024)S(1)}, f32[768]{0:T(1024)}, u32[]{:S(2)}) copy-start(f32[768]{0:T(1024)} %param.19) | copy-start | bytes 9220
  11.1 355.0 %reduce-scatter.3.cloned.1.call-start = ((), (), s32[]{:S(2)}) async-start(), calls=%async_computation.1 | async-start | bytes 14598144 | tf_op jit(solution)/shard_map/reduce_scatter | solution.py:630
  11.2 13.0 %collective-permute-start = (bf16[256,768]{1,0:T(8,128)(2,1)S(1)}, bf16[256,768]{1,0:T(8,128)(2,1)S(1)}, u32[]{:S(2)}, u32[]{:S(2)}) collective-permute-start(bf16[256,768]{1,0:T(8,128)(2,1)S(1)} %slice.204), channel_id=1, source_target_pairs={{0,8},{8,16},{16,24},{1,9},{9,17},{17,25},{2,10},{10,18},{18,26},{... | collective-permute-start | bytes 1179656 | tf_op jit(solution)/shard_map/ppermute | solution.py:571
  204.5 1.1 copy-start.1
  204.5 1.4 copy-start.10
  204.5 2.7 copy-start.3
  204.5 3.0 copy-start.9
  204.5 5.3 %copy-start.2 = (f32[512,768]{1,0:T(8,128)S(1)}, f32[512,768]{1,0:T(8,128)}, u32[]{:S(2)}) copy-start(f32[512,768]{1,0:T(8,128)} %get-tuple-element.44) | copy-start | bytes 4718596
  204.5 5.3 %copy-start.5 = (f32[768]{0:T(1024)S(1)}, f32[768]{0:T(1024)}, u32[]{:S(2)}) copy-start(f32[768]{0:T(1024)} %param.18) | copy-start | bytes 9220
  205.9 3.9 %collective-permute-start.1 = (bf16[256,768]{1,0:T(8,128)(2,1)S(1)}, bf16[256,768]{1,0:T(8,128)(2,1)S(1)}, u32[]{:S(2)}, u32[]{:S(2)}) collective-permute-start(bf16[256,768]{1,0:T(8,128)(2,1)S(1)} %copy-done.10), channel_id=1, source_target_pairs={{8,0},{16,8},{24,16},{9,1},{17,9},{25,17},{10,2},{18,10},{26,18},{... | collective-permute-start | bytes 1179656 | tf_op jit(solution)/shard_map/ppermute | solution.py:590
Sparse Core Ops, SparseCore 0:
  11.5 105.2 all-gather.3
  204.7 161.3 reduce-scatter.2

commit v3 on v2

--- a/solution.py
+++ b/solution.py
@@ -313,29 +313,164 @@
     lax.fori_loop(0, count, one, 0)
 
 
+MESH = pl.DeviceIdType.MESH
+
+
+def meet_all():
+    barrier = pltpu.get_barrier_semaphore()
+    others = 0
+    for axis in ("batch", "mp"):
+        size = lax.axis_size(axis)
+        for by in range(1, size):
+            other = lax.rem(lax.axis_index(axis) + by, size)
+            pl.semaphore_signal(barrier, inc=1, device_id={axis: other}, device_id_type=MESH)
+        others += size - 1
+    pl.semaphore_wait(barrier, others)
+
+
+class Place:
+    def __init__(self):
+        self.b = lax.axis_index("batch")
+        self.m = lax.axis_index("mp")
+        self.zs = lax.axis_size("batch") // 2
+        self.z = self.b // 2
+        self.y = lax.rem(self.b, 2)
+
+    def behind(self, k):
+        return lax.rem(self.z + self.zs - k, self.zs) * 2
+
+    def ahead(self, k):
+        return lax.rem(self.z + k, self.zs) * 2
+
+    def flip_x(self):
+        return lax.rem(self.m + 2, 4)
+
+    def flip_core(self, m):
+        return m + 1 - 2 * lax.rem(m, 2)
+
+
+class Gather:
+    def __init__(self, pieces, w, send_sems, recv_sems, own_sems):
+        self.pieces, self.w, self.send, self.recv, self.own = pieces, w, send_sems, recv_sems, own_sems
+        self.at = Place()
+        self.shard = pieces.shape[1]
+        self.half = self.shard // 2
+
+    def spot(self, p, c, k, j, core=False):
+        at = self.at
+        cross_y = j in ((1, 3) if c == 0 else (2, 3))
+        cross_x = j in ((2, 3) if c == 0 else (1, 3))
+        b = at.behind(k) + (1 - at.y if cross_y else at.y)
+        m = at.flip_x() if cross_x else at.m
+        m = at.flip_core(m) if core else m
+        first = pl.multiple_of(b * self.shard + c * self.half, 16)
+        return self.w.at[p, m, pl.ds(first, self.half), :]
+
+    def copy(self, p, c, k, j, number, target, core=False):
+        own = self.pieces.at[p, c * self.half : (c + 1) * self.half, :]
+        return pltpu.make_async_remote_copy(
+            own if (k, j) == (0, 0) else self.spot(p, c, k, j),
+            self.spot(p, c, k, j),
+            self.send.at[p, c, number],
+            self.recv.at[p, c, number],
+            device_id=target,
+            device_id_type=MESH,
+        )
+
+    def to(self, axis):
+        at = self.at
+        return {"batch": at.z * 2 + 1 - at.y} if axis == "y" else {"mp": at.flip_x()}
+
+    def hops(self, p, c, k, j):
+        zs = self.at.zs
+        axes = ("y", "x") if c == 0 else ("x", "y")
+        out = []
+        if (k, j) == (0, 0):
+            for by in range(1, zs):
+                out.append(self.copy(p, c, k, j, by - 1, {"batch": self.at.ahead(by) + self.at.y}))
+        if j == 0:
+            out.append(self.copy(p, c, k, j, zs - 1 + k, self.to(axes[0])))
+        if j in (0, 1):
+            out.append(self.copy(p, c, k, j, 2 * zs - 1 + 2 * k + j, self.to(axes[1])))
+        out.append(self.copy(p, c, k, j, 4 * zs - 1 + 4 * k + j, {"mp": self.at.flip_core(self.at.m)}))
+        return out
+
+    def arrived(self, p, c, k, j):
+        zs = self.at.zs
+        number = (k - 1, zs - 1 + k, 2 * zs - 1 + 2 * k, 2 * zs + 2 * k)[j]
+        self.wait(p, c, number, self.spot(p, c, k, j))
+
+    def wait(self, p, c, number, ref):
+        pltpu.make_async_copy(ref, ref, self.recv.at[p, c, number]).wait()
+
+    def begin(self, p):
+        own = self.w.at[p, self.at.m, pl.ds(pl.multiple_of(self.at.b * self.shard, 16), self.shard), :]
+        pltpu.make_async_copy(self.pieces.at[p], own, self.own.at[p]).start()
+        for c in range(2):
+            for hop in self.hops(p, c, 0, 0):
+                hop.start()
+
+    def relay(self, p, c, k, j):
+        self.arrived(p, c, k, j)
+        for hop in self.hops(p, c, k, j):
+            hop.start()
+
+    def relay_all(self, p):
+        for j in range(4):
+            for k in range(self.at.zs):
+                for c in range(2):
+                    if (k, j) != (0, 0):
+                        self.relay(p, c, k, j)
+
+    def finish(self, p):
+        own = self.w.at[p, self.at.m, pl.ds(pl.multiple_of(self.at.b * self.shard, 16), self.shard), :]
+        pltpu.make_async_copy(self.pieces.at[p], own, self.own.at[p]).wait()
+        for k in range(self.at.zs):
+            for j in range(4):
+                for c in range(2):
+                    self.wait(p, c, 4 * self.at.zs - 1 + 4 * k + j, self.spot(p, c, k, j, core=True))
+
+    def drain(self):
+        for p in range(3):
+            for c in range(2):
+                for k in range(self.at.zs):
+                    for j in range(4):
+                        for hop in self.hops(p, c, k, j):
+                            hop.wait_send()
+
+
 def layer_kernel(
-    wa_hbm, wu_hbm, wd_hbm, ext_ref, grad_ref, cols_ref, seg_row_ref, gains_ref, kernel_ref,
-    ga_hbm, gu_hbm, gd_hbm, out_ref, resid_grad_ref, own_ref, pass_ref, small_ref, gain_ref,
-    wa, wu, wd, ga, gu, gd, normed, proj, mixed, prob, heads, bias, wide, acc, resid, normed_two,
-    gffn_t, two_t, normed_t, hidden, upper, lower, in_sems, out_sems,
+    pieces_ref, tok_ref, grad_ref, cols_ref, seg_row_ref, gains_ref, kernel_ref,
+    g_hbm, out_ref, resid_grad_ref, own_ref, pass_ref, small_ref,
+    w, g, ext_ref, normed, proj, mixed, prob, heads, bias, wide, acc, resid, normed_two,
+    gffn_t, two_t, normed_t, hidden, upper, lower, send_sems, recv_sems, own_sems, halo_sems, out_sems,
 ):
-    parts = wa.shape[0]
+    parts = w.shape[1]
     rows, width = resid.shape
     span = HALO + rows
     tiles = rows // SEQ_MAX
     tile = SEQ_MAX
 
-    def fetch(hbm, ref, piece, m):
-        return pltpu.make_async_copy(hbm.at[m], ref.at[m], in_sems.at[piece, m])
-
-    def put(ref, hbm, piece, m):
-        return pltpu.make_async_copy(ref.at[m], hbm.at[m], out_sems.at[piece, m])
-
-    for m in range(parts):
-        fetch(wa_hbm, wa, 0, m).start()
-    for m in range(parts):
-        fetch(wu_hbm, wu, 1, m).start()
-        fetch(wd_hbm, wd, 2, m).start()
+    wa, wu, wd = w.at[0], w.at[1], w.at[2]
+    ga, gu, gd = g.at[0], g.at[1], g.at[2]
+    pull = Gather(pieces_ref, w, send_sems, recv_sems, own_sems)
+
+    def put(piece, m):
+        return pltpu.make_async_copy(g.at[piece, m], g_hbm.at[piece, m], out_sems.at[piece, m])
+
+    meet_all()
+    pass_on = pltpu.make_async_remote_copy(
+        tok_ref.at[rows - HALO :],
+        ext_ref.at[:HALO],
+        halo_sems.at[0],
+        halo_sems.at[1],
+        device_id={"mp": lax.rem(lax.axis_index("mp") + 1, parts)},
+        device_id_type=MESH,
+    )
+    pass_on.start()
+    for p in range(3):
+        pull.begin(p)
+    ext_ref[HALO:, :] = tok_ref[...]
 
     gain_one = gains_ref[0:1, :]
     gain_two = gains_ref[1:2, :]
@@ -344,6 +479,7 @@
         values = ext_ref[at, :].astype(F32)
         normed[at, :] = (values * rms(values) * gain_one).astype(BF16)
 
+    pass_on.wait()
     rows_loop(span, 128, norm_one)
     for at in range(tiles):
         key = lax.broadcasted_iota(jnp.int32, (2 * tile, tile), 0)
@@ -354,7 +490,6 @@
     acc[...] = jnp.zeros_like(acc)
 
     def forward(m):
-        fetch(wa_hbm, wa, 0, m).wait()
         wide[...] = nn(normed[...], wa[m, :, BLK:])
         for c in range(5):
             source = wide[:, blk(c)]
@@ -380,6 +515,10 @@
             heads[m, own_at, blk(1)] = outs[2].T.astype(BF16)
         acc[...] += nt(heads[m], wa[m, :, : 2 * BLK])
 
+    for p in range(3):
+        pull.relay_all(p)
+    for p in range(3):
+        pull.finish(p)
     parts_loop(parts, forward)
 
     def middle(at):
@@ -399,22 +538,20 @@
     own_ref[...] = jnp.zeros_like(own_ref)
 
     def feed(m):
-        fetch(wu_hbm, wu, 1, m).wait()
-        fetch(wd_hbm, wd, 2, m).wait()
         up = jnp.maximum(nn(normed_two[...], wu[m]), 0.0)
         upper[...] = (2.0 * up).astype(BF16)
         hidden[...] = (up * up).astype(BF16)
         acc[...] += nt(hidden[...], wd[m])
         gd[m] = nn(gffn_t[...], hidden[...]).astype(BF16)
-        put(gd, gd_hbm, 2, m).start()
+        put(2, m).start()
         lower[...] = (nn(gffn[...], wd[m]) * upper[...].astype(F32)).astype(BF16)
         gu[m] = nn(two_t[...], lower[...]).astype(BF16)
-        put(gu, gu_hbm, 1, m).start()
+        put(1, m).start()
         own_ref[...] += nt(lower[...], wu[m])
 
     parts_loop(parts, feed)
 
-    gain_ref[...] = jnp.zeros_like(gain_ref)
+    small_ref[...] = jnp.zeros_like(small_ref)
 
     def turn(at):
         value = resid[at, :]
@@ -422,7 +559,7 @@
         scale = rms(value)
         hat = value * scale
         grad = own_ref[at, :]
-        gain_ref[0:1, :] += jnp.sum(grad * hat, axis=0, keepdims=True)
+        small_ref[0, 4:5, :] += jnp.sum(grad * hat, axis=0, keepdims=True)
         total = grad_ref[at, :].astype(F32) + rms_back(grad, gain_two, hat, scale)
         resid_grad_ref[at, :] = total
         out_ref[at, :] = (value + filled * acc[at, :]).astype(BF16)
@@ -459,9 +596,9 @@
             one = grad * cols_ref[:, 0:1]
             two = grad * cols_ref[:, 1:2]
             source = proj[m, :, blk(c)].astype(F32)
-            small_ref[m, 0:1, blk(c)] = jnp.sum(grad * source, axis=0, keepdims=True)
-            small_ref[m, 1:2, blk(c)] = jnp.sum(one * pltpu.roll(source, 1, 0), axis=0, keepdims=True)
-            small_ref[m, 2:3, blk(c)] = jnp.sum(two * pltpu.roll(source, 2, 0), axis=0, keepdims=True)
+            small_ref[m, 0:1, blk(c + 1)] = jnp.sum(grad * source, axis=0, keepdims=True)
+            small_ref[m, 1:2, blk(c + 1)] = jnp.sum(one * pltpu.roll(source, 1, 0), axis=0, keepdims=True)
+            small_ref[m, 2:3, blk(c + 1)] = jnp.sum(two * pltpu.roll(source, 2, 0), axis=0, keepdims=True)
             mixed[m, :, blk(c)] = (
                 kernel_ref[m, 0:1, blk(c)] * grad
                 + kernel_ref[m, 1:2, blk(c)] * pltpu.roll(one, span - 1, 0)
@@ -472,41 +609,52 @@
         ga[m, :, blk(0)] = part[:, blk(0)].astype(BF16)
         ga[m, :, blk(1)] = (half_of(part[:, blk(1)], False) + half_of(whole[:, blk(0)], True)).astype(BF16)
         ga[m, :, 2 * BLK :] = whole[:, BLK:].astype(BF16)
-        put(ga, ga_hbm, 0, m).start()
+        put(0, m).start()
         own_ref[...] += nt(mixed[m, HALO:, :], wa[m, :, BLK:])
         acc[:HALO, :] += nt(mixed[m, :HALO, :], wa[m, :, BLK:])
 
     parts_loop(parts, backward)
     pass_ref[...] = acc[:HALO, :].astype(BF16)
+
+    def gain_rows(at, grad):
+        values = ext_ref[at, :].astype(F32)
+        small_ref[0, 3:4, :] += jnp.sum(grad * (values * rms(values)), axis=0, keepdims=True)
+
+    rows_loop(HALO, 128, lambda at: gain_rows(at, acc[at, :]))
+    rows_loop(rows, 128, lambda at: gain_rows(pl.ds(at.start + HALO, at.size), own_ref[at, :]))
+    for m in range(1, parts):
+        small_ref[m, 3:5, :] = small_ref[0, 3:5, :]
+    pull.drain()
     for m in range(parts):
-        put(ga, ga_hbm, 0, m).wait()
-        put(gu, gu_hbm, 1, m).wait()
-        put(gd, gd_hbm, 2, m).wait()
-
-
-def layer_call(wa, wu, wd, ext, grad_out, cols, seg_row, gains, kernel):
-    parts, width, _ = wa.shape
-    rows = grad_out.shape[0]
+        put(0, m).wait()
+        put(1, m).wait()
+        put(2, m).wait()
+
+
+def layer_call(pieces, tokens, grad_out, cols, seg_row, gains, kernel):
+    parts = lax.axis_size("mp")
+    rows, width = grad_out.shape
     span = rows + HALO
     tiles = rows // SEQ_MAX
+    copies = 8 * (lax.axis_size("batch") // 2) - 1
     vmem = pl.BlockSpec(memory_space=pltpu.VMEM)
     hbm = pl.BlockSpec(memory_space=pl.ANY)
-    big = pltpu.VMEM((parts, width, width), BF16)
+    big = pltpu.VMEM((3, parts, width, width), BF16)
     return pl.pallas_call(
         layer_kernel,
-        in_specs=[hbm] * 3 + [vmem] * 6,
-        out_specs=[hbm] * 3 + [vmem] * 6,
-        out_shape=[jax.ShapeDtypeStruct((parts, width, width), BF16)] * 3
-        + [
+        in_specs=[vmem] * 7,
+        out_specs=[hbm] + [vmem] * 5,
+        out_shape=[
+            jax.ShapeDtypeStruct((3, parts, width, width), BF16),
             jax.ShapeDtypeStruct((rows, width), BF16),
             jax.ShapeDtypeStruct((rows, width), F32),
             jax.ShapeDtypeStruct((rows, width), F32),
             jax.ShapeDtypeStruct((HALO, width), BF16),
-            jax.ShapeDtypeStruct((parts, 3, COLUMNS), F32),
-            jax.ShapeDtypeStruct((1, width), F32),
+            jax.ShapeDtypeStruct((parts, 8, width), F32),
         ],
         scratch_shapes=[
-            big, big, big, big, big, big,
+            big, big,
+            pltpu.VMEM((span, width), BF16),
             pltpu.VMEM((span, width), BF16),
             pltpu.VMEM((parts, span, COLUMNS), BF16),
             pltpu.VMEM((parts, span, COLUMNS), BF16),
@@ -523,12 +671,271 @@
             pltpu.VMEM((rows, width), BF16),
             pltpu.VMEM((rows, width), BF16),
             pltpu.VMEM((rows, width), BF16),
+            pltpu.SemaphoreType.DMA((3, 2, copies)),
+            pltpu.SemaphoreType.DMA((3, 2, copies)),
+            pltpu.SemaphoreType.DMA((3,)),
+            pltpu.SemaphoreType.DMA((2,)),
             pltpu.SemaphoreType.DMA((3, parts)),
-            pltpu.SemaphoreType.DMA((3, parts)),
-        ],
-        compiler_params=pltpu.CompilerParams(vmem_limit_bytes=67043328),
+        ],
+        compiler_params=pltpu.CompilerParams(
+            vmem_limit_bytes=67043328, collective_id=0, has_side_effects=True
+        ),
         name="layer",
-    )(wa, wu, wd, ext, grad_out, cols, seg_row, gains, kernel)
+    )(pieces, tokens, grad_out, cols, seg_row, gains, kernel)
+
+
+class Reduce:
+    def __init__(self, g_hbm, g, one, two, three, four, sems):
+        self.g_hbm, self.g, self.one, self.two, self.three, self.four, self.sems = g_hbm, g, one, two, three, four, sems
+        self.at = Place()
+        self.x = self.at.m // 2
+        self.core = lax.rem(self.at.m, 2)
+        self.half = g.shape[4] // 2
+
+    def z(self, k):
+        return self.at.ahead(k) // 2
+
+    def lanes(self, c):
+        return slice(c * self.half, (c + 1) * self.half)
+
+    def remote(self, source, target, number, device):
+        return pltpu.make_async_remote_copy(
+            source,
+            target,
+            self.sems.at[(0,) + number],
+            self.sems.at[(1,) + number],
+            device_id=device,
+            device_id_type=MESH,
+        )
+
+    def load(self, p, k):
+        z = self.z(k)
+        return pltpu.make_async_copy(self.g_hbm.at[p, :, self.core, z], self.g.at[p, :, z], self.sems.at[0, p, k, 7])
+
+    def first(self, p, k):
+        other = {"mp": self.at.flip_core(self.at.m)}
+        return self.remote(self.g_hbm.at[p, :, 1 - self.core, self.z(k)], self.one.at[p, k], (p, k, 0), other)
+
+    def second(self, p, k, c):
+        z, at = self.z(k), self.at
+        if c == 0:
+            source, device = self.g.at[p, 1 - self.x, z, :, self.lanes(0), :], {"mp": at.flip_x()}
+        else:
+            source = self.g.at[p, :, z, 1 - at.y, self.lanes(1), :]
+            device = {"batch": at.z * 2 + 1 - at.y}
+        return self.remote(source, self.two.at[p, k, c], (p, k, 1 + c), device)
+
+    def third(self, p, k, c):
+        z, at = self.z(k), self.at
+        if c == 0:
+            source, device = self.g.at[p, self.x, z, 1 - at.y, self.lanes(0), :], {"batch": at.z * 2 + 1 - at.y}
+        else:
+            source, device = self.g.at[p, 1 - self.x, z, at.y, self.lanes(1), :], {"mp": at.flip_x()}
+        return self.remote(source, self.three.at[p, k, c], (p, k, 3 + c), device)
+
+    def fourth(self, p, k, c):
+        at = self.at
+        source = self.g.at[p, self.x, self.z(k), at.y, self.lanes(c), :]
+        return self.remote(source, self.four.at[p, k - 1, c], (p, k, 5 + c), {"batch": at.ahead(k) + at.y})
+
+    def start(self, p, k):
+        self.load(p, k).start()
+        self.first(p, k).start()
+
+    def step_one(self, p, k):
+        z = self.z(k)
+        self.load(p, k).wait()
+        self.first(p, k).wait_recv()
+        for x in range(2):
+            self.g[p, x, z] += self.one[p, k, x]
+        for c in range(2):
+            self.second(p, k, c).start()
+
+    def step_two(self, p, k):
+        z, at = self.z(k), self.at
+        self.second(p, k, 0).wait_recv()
+        for y in range(2):
+            self.g[p, self.x, z, y, self.lanes(0), :] += self.two[p, k, 0, y]
+        self.third(p, k, 0).start()
+        self.second(p, k, 1).wait_recv()
+        for x in range(2):
+            self.g[p, x, z, at.y, self.lanes(1), :] += self.two[p, k, 1, x]
+        self.third(p, k, 1).start()
+
+    def step_three(self, p, k):
+        z, at = self.z(k), self.at
+        for c in range(2):
+            self.third(p, k, c).wait_recv()
+            self.g[p, self.x, z, at.y, self.lanes(c), :] += self.three[p, k, c]
+            if k:
+                self.fourth(p, k, c).start()
+
+    def step_four(self, p, out):
+        for c in range(2):
+            total = self.g[p, self.x, self.at.z, self.at.y, self.lanes(c), :].astype(F32)
+            for k in range(1, self.at.zs):
+                self.fourth(p, k, c).wait_recv()
+                total = total + self.four[p, k - 1, c].astype(F32)
+            out[p, self.lanes(c), :] = total
+
+    def drain(self, p, k):
+        self.first(p, k).wait_send()
+        for c in range(2):
+            self.second(p, k, c).wait_send()
+            self.third(p, k, c).wait_send()
+            if k:
+                self.fourth(p, k, c).wait_send()
+
+
+class Small:
+    def __init__(self, source, one, two, three, sums, sems):
+        self.source, self.one, self.two, self.three, self.sums, self.sems = source, one, two, three, sums, sems
+        self.at = Place()
+        self.x = self.at.m // 2
+        self.core = lax.rem(self.at.m, 2)
+        self.count = lax.axis_size("batch")
+
+    def remote(self, source, target, number, device):
+        return pltpu.make_async_remote_copy(
+            source, target, self.sems.at[0, number], self.sems.at[1, number], device_id=device, device_id_type=MESH
+        )
+
+    def core_copy(self, x):
+        device = {"mp": self.at.flip_core(self.at.m)}
+        return self.remote(self.source.at[x * 2 + 1 - self.core], self.one.at[x], x, device)
+
+    def x_copy(self):
+        return self.remote(self.sums.at[1 - self.x], self.two, 2, {"mp": self.at.flip_x()})
+
+    def far_copy(self, by):
+        other = lax.rem(self.at.b + by, self.count)
+        return self.remote(self.sums.at[self.x], self.three.at[by - 1], 2 + by, {"batch": other})
+
+    def begin(self):
+        for x in range(2):
+            self.core_copy(x).start()
+
+    def middle(self):
+        for x in range(2):
+            self.core_copy(x).wait_recv()
+            self.sums[x] = self.source[x * 2 + self.core] + self.one[x]
+        self.x_copy().start()
+
+    def later(self):
+        self.x_copy().wait_recv()
+        self.sums[self.x] += self.two[...]
+        for by in range(1, self.count):
+            self.far_copy(by).start()
+
+    def finish(self, out):
+        total = self.sums[self.x]
+        for by in range(1, self.count):
+            self.far_copy(by).wait_recv()
+            total = total + self.three[by - 1]
+        out[...] = total
+        for x in range(2):
+            self.core_copy(x).wait_send()
+        self.x_copy().wait_send()
+        for by in range(1, self.count):
+            self.far_copy(by).wait_send()
+
+
+def reduce_kernel(
+    g_hbm, small_ref, pass_ref, resid_grad_ref, own_ref, tok_ref, gains_ref, own_out, tokens_out, small_out,
+    g, one, two, three, four, passed, s_sums, s_one, s_two, s_three, sems, small_sems, pass_sems,
+):
+    parts = lax.axis_size("mp")
+    rows = tok_ref.shape[0]
+    meet_all()
+    push = Reduce(g_hbm, g, one, two, three, four, sems)
+    small = Small(small_ref, s_one, s_two, s_three, s_sums, small_sems)
+    me = lax.axis_index("mp")
+    pass_on = pltpu.make_async_remote_copy(
+        pass_ref,
+        passed,
+        pass_sems.at[0],
+        pass_sems.at[1],
+        device_id={"mp": lax.rem(me + parts - 1, parts)},
+        device_id_type=MESH,
+    )
+    zs = push.at.zs
+    chunks = [(p, k) for p in (2, 1, 0) for k in [*range(1, zs), 0]]
+    for chunk in chunks[:4]:
+        push.start(*chunk)
+    small.begin()
+    pass_on.start()
+    for chunk in chunks[4:]:
+        push.start(*chunk)
+
+    def last(at, extra):
+        values = tok_ref[at, :].astype(F32)
+        scale = rms(values)
+        tokens_out[at, :] = resid_grad_ref[at, :] + rms_back(
+            own_ref[at, :] + extra, gains_ref[0:1, :], values * scale, scale
+        )
+
+    def end_rows(at):
+        keep = jnp.where(me < parts - 1, 1.0, 0.0)
+        last(pl.ds(at.start + rows - HALO, at.size), passed[at, :].astype(F32) * keep)
+
+    for n in range(len(chunks) + 4):
+        if n < len(chunks):
+            push.step_one(*chunks[n])
+        if 0 <= n - 2 < len(chunks):
+            push.step_two(*chunks[n - 2])
+        if 0 <= n - 4 < len(chunks):
+            p, k = chunks[n - 4]
+            push.step_three(p, k)
+            if k == 0 and p != 2:
+                push.step_four(p + 1, own_out)
+        if n == 1:
+            small.middle()
+        if n == 3:
+            small.later()
+            pass_on.wait()
+            rows_loop(rows - HALO, 128, lambda at: last(at, 0.0))
+            rows_loop(HALO, 128, end_rows)
+    push.step_four(0, own_out)
+    small.finish(small_out)
+    for chunk in chunks:
+        push.drain(*chunk)
+
+
+def reduce_call(g_hbm, small, passed, resid_grad, own, tokens, gains):
+    rows, width = tokens.shape
+    zs = lax.axis_size("batch") // 2
+    shard = width // (2 * zs)
+    half = shard // 2
+    vmem = pl.BlockSpec(memory_space=pltpu.VMEM)
+    return pl.pallas_call(
+        reduce_kernel,
+        in_specs=[pl.BlockSpec(memory_space=pl.ANY)] + [vmem] * 6,
+        out_specs=[vmem] * 3,
+        out_shape=[
+            jax.ShapeDtypeStruct((3, shard, width), F32),
+            jax.ShapeDtypeStruct((rows, width), F32),
+            jax.ShapeDtypeStruct((8, width), F32),
+        ],
+        scratch_shapes=[
+            pltpu.VMEM((3, 2, zs, 2, shard, width), BF16),
+            pltpu.VMEM((3, zs, 2, 2, shard, width), BF16),
+            pltpu.VMEM((3, zs, 2, 2, half, width), BF16),
+            pltpu.VMEM((3, zs, 2, half, width), BF16),
+            pltpu.VMEM((3, zs - 1, 2, half, width), BF16),
+            pltpu.VMEM((HALO, width), BF16),
+            pltpu.VMEM((2, 8, width), F32),
+            pltpu.VMEM((2, 8, width), F32),
+            pltpu.VMEM((8, width), F32),
+            pltpu.VMEM((2 * zs - 1, 8, width), F32),
+            pltpu.SemaphoreType.DMA((2, 3, zs, 8)),
+            pltpu.SemaphoreType.DMA((2, 2 + 2 * zs)),
+            pltpu.SemaphoreType.DMA((2,)),
+        ],
+        compiler_params=pltpu.CompilerParams(
+            vmem_limit_bytes=60 * 1024 * 1024, collective_id=1, has_side_effects=True
+        ),
+        name="reduce",
+    )(g_hbm.reshape(3, 2, 2, zs, 2, shard, width), small, passed, resid_grad, own, tokens, gains)
 
 
 def arrange(q, k, v, o):
@@ -554,7 +961,8 @@
     shard = w_qkv.shape[0]
     fits = (
         rows % SEQ_MAX == 0 and part == 3 * HD and width == 4 * part and shard % 16 == 0
-        and w_up.shape[1] == width and seg_ids.shape[0] == n_mp * rows
+        and w_up.shape[1] == width and seg_ids.shape[0] == n_mp * rows and shard % 32 == 0 and n_batch % 2 == 0
+        and rows + HALO == width
     )
     if not fits:
         return shards_plain(
@@ -563,12 +971,9 @@
     own_start = lax.axis_index("mp") * rows
     piece_a = arrange(w_qkv[:, 0], w_qkv[:, 1], w_qkv[:, 2], w_out.T)
     pieces = jnp.stack([piece_a, w_up, w_down.T])
-    wa, wu, wd = gather(pieces)
     taps = lax.all_gather(dconv_kernel, "mp", axis=0, tiled=False)
     zero = jnp.zeros_like(taps[:, 0])
     kernel = arrange(taps[:, 0], taps[:, 1], taps[:, 2], zero)[..., BLK:]
-    back = [(i, i + 1) for i in range(n_mp - 1)]
-    ext = jnp.concatenate([lax.ppermute(tokens[rows - HALO :], "mp", back), tokens], axis=0)
     seg_pad = jnp.concatenate([jnp.full((HALO,), -1, jnp.int32), seg_ids])
     seg = lax.dynamic_slice_in_dim(seg_pad, own_start, HALO + rows, 0).astype(F32)
     slot = own_start - HALO + lax.iota(jnp.int32, HALO + rows)
@@ -582,52 +987,27 @@
         axis=1,
     )
     gains = jnp.stack([gain_attn, gain_ffn])
-    ga, gu, gd, layer_out, resid_grad, own_normed, passed, taps_grad, gain_two = layer_call(
-        wa, wu, wd, ext, grad_out, cols, seg[None, HALO:], gains, kernel
-    )
-    own = scatter(ga, gu, gd)
-    ahead = [(i + 1, i) for i in range(n_mp - 1)]
-    passed = lax.ppermute(passed, "mp", ahead).astype(F32)
-    own_normed = own_normed + jnp.pad(passed, ((rows - HALO, 0), (0, 0)))
-    values = tokens.astype(F32)
-    scale = rms(values)
-    hat = values * scale
-    grad_tokens = resid_grad + rms_back(own_normed, gain_attn, hat, scale)
-    gain_one = jnp.sum(own_normed * hat, axis=0)
-    first, second, third, _ = disarrange(jnp.pad(taps_grad, ((0, 0), (0, 0), (BLK, 0))))
-    small = jnp.stack([first, second, third]).transpose(0, 2, 1, 3).reshape(9, width)
-    small = jnp.concatenate([small, gain_one[None], gain_two])
-    piece = width // (n_mp * n_batch)
-    small = small.reshape(11, n_mp * n_batch, piece).transpose(1, 0, 2)
-    small = lax.psum_scatter(small, ("mp", "batch"), scatter_dimension=0, tiled=False)
+    g, layer_out, resid_grad, own_normed, passed, small = layer_call(
+        pieces, tokens, grad_out, cols, seg[None, HALO:], gains, kernel
+    )
+    own, grad_tokens, small = reduce_call(g, small, passed, resid_grad, own_normed, tokens, gains)
+    first, second, third, _ = disarrange(small[:3])
+    piece = part // n_batch
+    at_piece = lax.axis_index("batch") * piece
+    taps_grad = lax.dynamic_slice_in_dim(jnp.stack([first, second, third]), at_piece, piece, 2)
+    gain_grads = lax.dynamic_slice_in_dim(small[3:5], lax.axis_index("mp") * part + at_piece, piece, 1)
     q, k, v, o = disarrange(own[0])
     return (
         layer_out,
         grad_tokens,
-        small[9],
-        small[10],
+        gain_grads[0],
+        gain_grads[1],
         jnp.stack([q, k, v], axis=1),
-        small[:9].reshape(3, 3, piece),
+        taps_grad,
         o.T,
         own[1],
         own[2].T,
     )
-
-
-def gather(pieces):
-    full = lax.all_gather(pieces, ("batch", "mp"), axis=0, tiled=False)
-    n_mp = lax.axis_size("mp")
-    full = full.reshape((-1, n_mp) + pieces.shape).transpose(2, 1, 0, 3, 4)
-    full = full.reshape(3, n_mp, -1, pieces.shape[2])
-    return full[0], full[1], full[2]
-
-
-def scatter(ga, gu, gd):
-    n_mp, width, columns = ga.shape
-    n_batch = lax.axis_size("batch")
-    grads = jnp.stack([ga, gu, gd]).reshape(3, n_mp, n_batch, width // n_batch, columns)
-    grads = grads.transpose(2, 1, 0, 3, 4).reshape((-1, 3, width // n_batch, columns))
-    return lax.psum_scatter(grads, ("batch", "mp"), scatter_dimension=0, tiled=False).astype(F32)
 
 
 def solution(mesh):

time: 377 us -> 243 us (0.64)
  waiting for transfers between devices: 199 us -> 0 us
  Pallas kernels: 63.2 us -> 215 us
  blocking collectives: 52.7 us -> 6.44 us
  between operations: 15.1 us -> 1.49 us
  local copies, waits for them, and re-layouts: 26.7 us -> 14.1 us
  other arithmetic: 16.2 us -> 5.4 us
  starting transfers between devices: 3.79 us -> 0 us
    pallas_call x1 -> x2, Pallas kernels: 63.2 us -> 215 us  [the longest x1 137 us: layer_call(): pl.pallas_call(layer_kernel, in_specs=[vmem] * 7, out_specs=[hbm] + [vmem...]
    reduce_scatter x1 -> x0, waiting for transfers between devices: 105 us -> none  [scatter(): lax.psum_scatter(grads, ('batch', 'mp'), scatter_dimension=0, tiled=False)]
    all_gather x1 -> x0, waiting for transfers between devices: 91.5 us -> none  [gather(): full = lax.all_gather(pieces, ('batch', 'mp'), axis=0, tiled=False)]
    unnamed x1 -> x0, blocking collectives: 46.2 us -> none
    reshape x2 -> x0, local copies, waits for them, and re-layouts: 7.36 us -> none  [the longest x1 6.76 us: gather(): full = full.reshape((-1, n_mp) + pieces.shape).transpose(2, 1, 0, 3, 4)]
    transpose x3 -> x0, other arithmetic: 6.73 us -> none  [the longest x1 6.7 us: scatter(): grads.transpose(2, 1, 0, 3, 4).reshape((-1, 3, width // n_batch, columns))]
    transpose x3 -> x1, local copies, waits for them, and re-layouts: 5.65 us -> 0.02 us  [shards(): return (layer_out, grad_tokens, gain_grads[0], gain_grads[1], jnp.stack([...]
    slice x3 -> x1, local copies, waits for them, and re-layouts: 5.53 us -> 0.74 us  [shards(): small[3:5]]
  transfers between devices with their start and end apart: 4 -> 0, of which waited for: 3 -> 0; matrix products, arithmetic and copies ran while one was open for 3% -> 0% of each run, Pallas kernels for 0% -> 0%
where the time goes in v3:
time: 243 us; the launch traced here: 242 us
  Pallas kernels  215 us (88%)
  local copies, waits for them, and re-layouts  14.1 us (6%)
  blocking collectives  6.44 us (3%)
  other arithmetic  5.4 us (2%)
    pallas_call x1, Pallas kernels, layer_call(): pl.pallas_call(layer_kernel, in_specs=[vmem] * 7, out_specs=[hbm] + [vmem...  137 us
    pallas_call x1, Pallas kernels, reduce_call(): pl.pallas_call(reduce_kernel, in_specs=[pl.BlockSpec(memory_space=pl.ANY)...  77.4 us
    all_gather x1, blocking collectives, shards(): taps = lax.all_gather(dconv_kernel, 'mp', axis=0, tiled=False)  6.44 us

profile of v3, /device:TPU:0, one launch (start us, length us, event | category | flops | bytes accessed | tf_op | source)
XLA Modules:
  0.0 242.0 jit_solution(5531373710031090064)
XLA Ops:
  1.3 0.7 stack.75
  2.0 0.7 stack.76
  2.7 0.6 pad_maximum_fusion.3.gains_ref
  3.3 0.8 fusion.2
  4.1 0.6 slice.183
  4.7 0.8 fusion.4
  5.5 0.2 scatter.9
  5.7 6.4 %all-gather = f32[12,3,192]{2,1,0:T(4,128)S(1)} all-gather(f32[3,3,192]{2,1,0:T(4,128)} %param.21), channel_id=2, replica_groups=mesh['mp'=4,'batch'=8] {'mp'}, dimensions={0}, use_global_device_ids=true | all-gather | bytes 34560 | tf_op jit(solution)/shard_map/all_gather | solution.py:974
  12.2 0.7 concatenate.46.kernel_ref
  12.9 0.9 copy.30
  13.8 0.9 slice_bitcast_fusion.5
  14.7 0.1 concatenate.42
  14.8 1.8 pad_maximum_fusion.pieces_ref
  16.6 0.9 copy.34.cols_ref
  17.6 137.2 %layer.1 = (bf16[3,4,768,768]{3,2,1,0:T(8,128)(2,1)}, bf16[512,768]{1,0:T(8,128)(2,1)}, f32[512,768]{1,0:T(8,128)}, f32[512,768]{1,0:T(8,128)}, bf16[256,768]{1,0:T(8,128)(2,1)}, /*index=5*/f32[4,8,768]{2,1,0:T(8,128)}) custom-call(bf16[3,96,768]{2,1,0:T(8,128)(2,1)} %pad_maximum_fusion.pieces_ref, bf16[512,768]{1,0:T(8,128)(2,1)} %tok_ref.3, ...), custom_call_target="tpu_custom_call" | custom-call | tf_op jit(solution)/shard_map/layer/pallas_call | solution.py:643
  154.7 77.4 %reduce.5 = (f32[3,96,768]{2,1,0:T(8,128)}, f32[512,768]{1,0:T(8,128)}, f32[8,768]{1,0:T(8,128)}) custom-call(bf16[3,2,2,4,2,96,768]{6,5,4,3,2,1,0:T(8,128)(2,1)} %bitcast.57, f32[4,8,768]{2,1,0:T(8,128)} %get-tuple-element.44.small_ref, bf16[256,768]{1,0:T(8,128)(2,1)} %get-tuple-element.45.pass_ref, f32[512,768]{1,0:T(8,128)} %get-tuple-element.46.resid_grad_ref, ...), custom_call_target="tpu_custom_call" | custom-call | tf_op jit(solution)/shard_map/reduce/pallas_call | solution.py:910
  232.1 0.7 slice_bitcast_fusion.11
  232.8 0.7 fusion.7
  233.5 0.8 fusion.8
  234.3 0.7 slice.192
  235.0 0.1 constant_dynamic-slice_fusion
  235.1 0.7 fusion.1
  235.7 0.5 slice_bitcast_fusion.12
  236.3 0.0 copy-start.1
  236.3 2.1 slice_bitcast_fusion
  238.3 0.1 fusion.6
  238.5 0.0 copy-start
  238.5 0.7 copy.35
  239.2 0.7 pad_maximum_fusion.1
  240.0 0.0 copy-done.1
  240.0 0.9 copy.44
  240.9 0.0 copy-done
  240.9 1.1 copy.45
  (21 shorter events, 0.2 us)
Async XLA Ops:
  236.3 3.7 %copy-start.1 = (bf16[512,768]{1,0:T(8,128)(2,1)S(1)}, bf16[512,768]{1,0:T(8,128)(2,1)}, u32[]{:S(2)}) copy-start(bf16[512,768]{1,0:T(8,128)(2,1)} %get-tuple-element.114) | copy-start | bytes 2359300
  238.5 2.4 copy-start

commit v4 on v2

--- a/solution.py
+++ b/solution.py
@@ -313,29 +313,339 @@
     lax.fori_loop(0, count, one, 0)
 
 
+MESH = pl.DeviceIdType.MESH
+
+
+def meet_all():
+    barrier = pltpu.get_barrier_semaphore()
+    others = 0
+    for axis in ("batch", "mp"):
+        size = lax.axis_size(axis)
+        for by in range(1, size):
+            other = lax.rem(lax.axis_index(axis) + by, size)
+            pl.semaphore_signal(barrier, inc=1, device_id={axis: other}, device_id_type=MESH)
+        others += size - 1
+    pl.semaphore_wait(barrier, others)
+
+
+class Place:
+    def __init__(self):
+        self.b = lax.axis_index("batch")
+        self.m = lax.axis_index("mp")
+        self.zs = lax.axis_size("batch") // 2
+        self.z = self.b // 2
+        self.y = lax.rem(self.b, 2)
+
+    def behind(self, k):
+        return lax.rem(self.z + self.zs - k, self.zs) * 2
+
+    def ahead(self, k):
+        return lax.rem(self.z + k, self.zs) * 2
+
+    def flip_x(self):
+        return lax.rem(self.m + 2, 4)
+
+    def flip_core(self, m):
+        return m + 1 - 2 * lax.rem(m, 2)
+
+
+class Gather:
+    def __init__(self, pieces, w, send_sems, recv_sems, own_sems):
+        self.pieces, self.w, self.send, self.recv, self.own = pieces, w, send_sems, recv_sems, own_sems
+        self.at = Place()
+        self.shard = pieces.shape[1]
+        self.half = self.shard // 2
+
+    def spot(self, p, c, k, j, core=False):
+        at = self.at
+        cross_y = j in ((1, 3) if c == 0 else (2, 3))
+        cross_x = j in ((2, 3) if c == 0 else (1, 3))
+        b = at.behind(k) + (1 - at.y if cross_y else at.y)
+        m = at.flip_x() if cross_x else at.m
+        m = at.flip_core(m) if core else m
+        half = slice(c * self.half, (c + 1) * self.half)
+        return self.w.at[p, m // 2, lax.rem(m, 2), b // 2, lax.rem(b, 2), half, :]
+
+    def copy(self, p, c, k, j, number, target, core=False):
+        own = self.pieces.at[p, c * self.half : (c + 1) * self.half, :]
+        return pltpu.make_async_remote_copy(
+            own if (k, j) == (0, 0) else self.spot(p, c, k, j),
+            self.spot(p, c, k, j),
+            self.send.at[p, c, number],
+            self.recv.at[p, c, number],
+            device_id=target,
+            device_id_type=MESH,
+        )
+
+    def to(self, axis):
+        at = self.at
+        return {"batch": at.z * 2 + 1 - at.y} if axis == "y" else {"mp": at.flip_x()}
+
+    def along_z(self, p, c):
+        return [
+            self.copy(p, c, 0, 0, by - 1, {"batch": self.at.ahead(by) + self.at.y}) for by in range(1, self.at.zs)
+        ]
+
+    def hops(self, p, c, k, j):
+        zs = self.at.zs
+        axes = ("y", "x") if c == 0 else ("x", "y")
+        out = []
+        if j == 0:
+            out.append(self.copy(p, c, k, j, zs - 1 + k, self.to(axes[0])))
+        if j in (0, 1):
+            out.append(self.copy(p, c, k, j, 2 * zs - 1 + 2 * k + j, self.to(axes[1])))
+        out.append(self.copy(p, c, k, j, 4 * zs - 1 + 4 * k + j, {"mp": self.at.flip_core(self.at.m)}))
+        return out
+
+    def arrived(self, p, c, k, j):
+        zs = self.at.zs
+        number = (k - 1, zs - 1 + k, 2 * zs - 1 + 2 * k, 2 * zs + 2 * k)[j]
+        self.wait(p, c, number, self.spot(p, c, k, j))
+
+    def wait(self, p, c, number, ref):
+        pltpu.make_async_copy(ref, ref, self.recv.at[p, c, number]).wait()
+
+    def keep(self, p):
+        at = self.at
+        own = self.w.at[p, at.m // 2, lax.rem(at.m, 2), at.z, at.y]
+        return pltpu.make_async_copy(self.pieces.at[p], own, self.own.at[p])
+
+    def begin_z(self, p):
+        self.keep(p).start()
+        copies = [self.along_z(p, c) for c in range(2)]
+        for by in range(self.at.zs - 1):
+            for c in range(2):
+                copies[c][by].start()
+
+    def begin(self, p):
+        for c in range(2):
+            for hop in self.hops(p, c, 0, 0):
+                hop.start()
+
+    def relay(self, p, j):
+        for k in range(self.at.zs):
+            for c in range(2):
+                if (k, j) != (0, 0):
+                    self.arrived(p, c, k, j)
+                    for hop in self.hops(p, c, k, j):
+                        hop.start()
+
+    def finish(self, p):
+        self.keep(p).wait()
+        for k in range(self.at.zs):
+            for j in range(4):
+                for c in range(2):
+                    self.wait(p, c, 4 * self.at.zs - 1 + 4 * k + j, self.spot(p, c, k, j, core=True))
+
+    def drain(self, p):
+        for c in range(2):
+            for copy in self.along_z(p, c):
+                copy.wait_send()
+            for k in range(self.at.zs):
+                for j in range(4):
+                    for hop in self.hops(p, c, k, j):
+                        hop.wait_send()
+
+
+class Reduce:
+    def __init__(self, w, one, two, three, four, one_sems, sems):
+        self.w, self.one, self.two, self.three, self.four, self.one_sems, self.sems = (
+            w, one, two, three, four, one_sems, sems
+        )
+        self.at = Place()
+        self.x = self.at.m // 2
+        self.core = lax.rem(self.at.m, 2)
+        self.half = w.shape[5] // 2
+
+    def z(self, k):
+        return self.at.ahead(k) // 2
+
+    def lanes(self, c):
+        return slice(c * self.half, (c + 1) * self.half)
+
+    def remote(self, source, target, sems, number, device):
+        return pltpu.make_async_remote_copy(
+            source, target, sems.at[(0,) + number], sems.at[(1,) + number], device_id=device, device_id_type=MESH
+        )
+
+    def first(self, p, x):
+        other = {"mp": self.at.flip_core(self.at.m)}
+        return self.remote(self.w.at[p, x, 1 - self.core], self.one.at[p, x], self.one_sems, (p, x), other)
+
+    def second(self, p, k, c):
+        z, at = self.z(k), self.at
+        if c == 0:
+            source, device = self.w.at[p, 1 - self.x, self.core, z, :, self.lanes(0), :], {"mp": at.flip_x()}
+        else:
+            source = self.w.at[p, :, self.core, z, 1 - at.y, self.lanes(1), :]
+            device = {"batch": at.z * 2 + 1 - at.y}
+        return self.remote(source, self.two.at[p, k, c], self.sems, (p, k, c), device)
+
+    def third(self, p, k, c):
+        z, at = self.z(k), self.at
+        if c == 0:
+            source = self.w.at[p, self.x, self.core, z, 1 - at.y, self.lanes(0), :]
+            device = {"batch": at.z * 2 + 1 - at.y}
+        else:
+            source, device = self.w.at[p, 1 - self.x, self.core, z, at.y, self.lanes(1), :], {"mp": at.flip_x()}
+        return self.remote(source, self.three.at[p, k, c], self.sems, (p, k, 2 + c), device)
+
+    def fourth(self, p, k, c):
+        at = self.at
+        source = self.w.at[p, self.x, self.core, self.z(k), at.y, self.lanes(c), :]
+        return self.remote(source, self.four.at[p, k - 1, c], self.sems, (p, k, 4 + c), {"batch": at.ahead(k) + at.y})
+
+    def start(self, p):
+        for x in range(2):
+            self.first(p, x).start()
+
+    def met(self, p):
+        for x in range(2):
+            self.first(p, x).wait_recv()
+
+    def step_one(self, p, k):
+        z = self.z(k)
+        for x in range(2):
+            self.w[p, x, self.core, z] += self.one[p, x, z]
+        for c in range(2):
+            self.second(p, k, c).start()
+
+    def step_two(self, p, k):
+        z, at = self.z(k), self.at
+        self.second(p, k, 0).wait_recv()
+        for y in range(2):
+            self.w[p, self.x, self.core, z, y, self.lanes(0), :] += self.two[p, k, 0, y]
+        self.third(p, k, 0).start()
+        self.second(p, k, 1).wait_recv()
+        for x in range(2):
+            self.w[p, x, self.core, z, at.y, self.lanes(1), :] += self.two[p, k, 1, x]
+        self.third(p, k, 1).start()
+
+    def step_three(self, p, k):
+        z, at = self.z(k), self.at
+        for c in range(2):
+            self.third(p, k, c).wait_recv()
+            self.w[p, self.x, self.core, z, at.y, self.lanes(c), :] += self.three[p, k, c]
+            if k:
+                self.fourth(p, k, c).start()
+
+    def step_four(self, p, out):
+        for c in range(2):
+            total = self.w[p, self.x, self.core, self.at.z, self.at.y, self.lanes(c), :].astype(F32)
+            for k in range(1, self.at.zs):
+                self.fourth(p, k, c).wait_recv()
+                total = total + self.four[p, k - 1, c].astype(F32)
+            out[p, self.lanes(c), :] = total
+
+    def drain(self, p):
+        for x in range(2):
+            self.first(p, x).wait_send()
+        for k in range(self.at.zs):
+            for c in range(2):
+                self.second(p, k, c).wait_send()
+                self.third(p, k, c).wait_send()
+                if k:
+                    self.fourth(p, k, c).wait_send()
+
+
+class Small:
+    def __init__(self, source, one, two, three, sums, sems):
+        self.source, self.one, self.two, self.three, self.sums, self.sems = source, one, two, three, sums, sems
+        self.at = Place()
+        self.x = self.at.m // 2
+        self.core = lax.rem(self.at.m, 2)
+        self.count = lax.axis_size("batch")
+
+    def remote(self, source, target, number, device):
+        return pltpu.make_async_remote_copy(
+            source, target, self.sems.at[0, number], self.sems.at[1, number], device_id=device, device_id_type=MESH
+        )
+
+    def core_copy(self, x):
+        device = {"mp": self.at.flip_core(self.at.m)}
+        return self.remote(self.source.at[x * 2 + 1 - self.core], self.one.at[x], x, device)
+
+    def x_copy(self):
+        return self.remote(self.sums.at[1 - self.x], self.two, 2, {"mp": self.at.flip_x()})
+
+    def far_copy(self, by):
+        other = lax.rem(self.at.b + by, self.count)
+        return self.remote(self.sums.at[self.x], self.three.at[by - 1], 2 + by, {"batch": other})
+
+    def begin(self):
+        for x in range(2):
+            self.core_copy(x).start()
+
+    def middle(self):
+        for x in range(2):
+            self.core_copy(x).wait_recv()
+            self.sums[x] = self.source[x * 2 + self.core] + self.one[x]
+        self.x_copy().start()
+
+    def later(self):
+        self.x_copy().wait_recv()
+        self.sums[self.x] += self.two[...]
+        for by in range(1, self.count):
+            self.far_copy(by).start()
+
+    def finish(self, out):
+        total = self.sums[self.x]
+        for by in range(1, self.count):
+            self.far_copy(by).wait_recv()
+            total = total + self.three[by - 1]
+        out[...] = total
+        for x in range(2):
+            self.core_copy(x).wait_send()
+        self.x_copy().wait_send()
+        for by in range(1, self.count):
+            self.far_copy(by).wait_send()
+
+
 def layer_kernel(
-    wa_hbm, wu_hbm, wd_hbm, ext_ref, grad_ref, cols_ref, seg_row_ref, gains_ref, kernel_ref,
-    ga_hbm, gu_hbm, gd_hbm, out_ref, resid_grad_ref, own_ref, pass_ref, small_ref, gain_ref,
-    wa, wu, wd, ga, gu, gd, normed, proj, mixed, prob, heads, bias, wide, acc, resid, normed_two,
-    gffn_t, two_t, normed_t, hidden, upper, lower, in_sems, out_sems,
+    pieces_ref, tok_ref, grad_ref, cols_ref, seg_row_ref, gains_ref, kernel_ref,
+    out_ref, tokens_out, own_out, small_out,
+    w, ext_ref, normed, proj, mixed, prob, heads, bias, wide, acc, own_ref, normed_two,
+    gffn_t, two_t, hidden, upper, one, two, three, four, sent, passed,
+    small_ref, s_sums, s_one, s_two, s_three,
+    send_sems, recv_sems, own_sems, halo_sems, one_sems, sems, small_sems,
 ):
-    parts = wa.shape[0]
-    rows, width = resid.shape
+    parts = w.shape[1] * w.shape[2]
+    rows, width = tokens_out.shape
     span = HALO + rows
     tiles = rows // SEQ_MAX
     tile = SEQ_MAX
-
-    def fetch(hbm, ref, piece, m):
-        return pltpu.make_async_copy(hbm.at[m], ref.at[m], in_sems.at[piece, m])
-
-    def put(ref, hbm, piece, m):
-        return pltpu.make_async_copy(ref.at[m], hbm.at[m], out_sems.at[piece, m])
-
-    for m in range(parts):
-        fetch(wa_hbm, wa, 0, m).start()
-    for m in range(parts):
-        fetch(wu_hbm, wu, 1, m).start()
-        fetch(wd_hbm, wd, 2, m).start()
+    resid = tokens_out
+    me = lax.axis_index("mp")
+    pull = Gather(pieces_ref, w, send_sems, recv_sems, own_sems)
+    push = Reduce(w, one, two, three, four, one_sems, sems)
+    small = Small(small_ref, s_one, s_two, s_three, s_sums, small_sems)
+    zs = push.at.zs
+    ks = [*range(1, zs), 0]
+
+    def weight(piece, m):
+        return w[piece, m // 2, lax.rem(m, 2)].reshape(width, width)
+
+    def store(piece, m, lanes, value):
+        w[piece, m // 2, lax.rem(m, 2), :, :, :, lanes] = value.reshape(zs, 2, width // (2 * zs), value.shape[1])
+
+    def lanes_of(piece, m, lanes):
+        value = w[piece, m // 2, lax.rem(m, 2), :, :, :, lanes]
+        return value.reshape(width, value.shape[3])
+
+    def neighbour(source, target, first, by):
+        return pltpu.make_async_remote_copy(
+            source, target, halo_sems.at[first], halo_sems.at[first + 1],
+            device_id={"mp": lax.rem(me + by, parts)}, device_id_type=MESH,
+        )
+
+    meet_all()
+    pull.begin_z(0)
+    pull.begin(0)
+    pass_on = neighbour(tok_ref.at[rows - HALO :], ext_ref.at[:HALO], 0, 1)
+    pass_on.start()
+    pull.begin_z(1)
+    pull.begin_z(2)
+    ext_ref[HALO:, :] = tok_ref[...]
 
     gain_one = gains_ref[0:1, :]
     gain_two = gains_ref[1:2, :]
@@ -344,18 +654,18 @@
         values = ext_ref[at, :].astype(F32)
         normed[at, :] = (values * rms(values) * gain_one).astype(BF16)
 
+    pass_on.wait()
     rows_loop(span, 128, norm_one)
     for at in range(tiles):
         key = lax.broadcasted_iota(jnp.int32, (2 * tile, tile), 0)
         query = lax.broadcasted_iota(jnp.int32, (2 * tile, tile), 1) + tile
         seg_key = cols_ref[at * tile : (at + 2) * tile, 2:3]
         same = seg_key == seg_row_ref[0:1, at * tile : (at + 1) * tile]
-        bias[at] = jnp.where(same & (key <= query), 0.0, MASKED).astype(F32)
+        bias[at] = jnp.where(same & (key <= query), 0.0, MASKED).astype(BF16)
     acc[...] = jnp.zeros_like(acc)
 
     def forward(m):
-        fetch(wa_hbm, wa, 0, m).wait()
-        wide[...] = nn(normed[...], wa[m, :, BLK:])
+        wide[...] = nn(normed[...], lanes_of(0, m, slice(BLK, width)))
         for c in range(5):
             source = wide[:, blk(c)]
             proj[m, :, blk(c)] = source.astype(BF16)
@@ -370,7 +680,7 @@
             outs = []
             for h, (qb, kb, vb, qk_upper, v_upper, _) in enumerate(HEADS):
                 queries = half_of(mixed[m, query_at, blk(qb)], qk_upper) * jnp.asarray(HD**-0.5, BF16)
-                scores = nt(mixed[m, keys_at, blk(kb)], queries) + bias[at]
+                scores = nt(mixed[m, keys_at, blk(kb)], queries) + bias[at].astype(F32)
                 expo = jnp.exp(scores - jnp.max(scores, axis=0, keepdims=True))
                 share = (expo * (1.0 / jnp.sum(expo, axis=0, keepdims=True))).astype(BF16)
                 prob[m, at, h] = share
@@ -378,9 +688,27 @@
             own_at = slice(at * tile, (at + 1) * tile)
             heads[m, own_at, blk(0)] = (outs[0] + outs[1]).T.astype(BF16)
             heads[m, own_at, blk(1)] = outs[2].T.astype(BF16)
-        acc[...] += nt(heads[m], wa[m, :, : 2 * BLK])
-
+        acc[...] += nt(heads[m], lanes_of(0, m, slice(0, 2 * BLK)))
+
+        @pl.when(m == 1)
+        def _():
+            pull.relay(1, 1)
+            pull.begin(2)
+            pull.relay(2, 0)
+
+        @pl.when(m == 2)
+        def _():
+            pull.relay(1, 2)
+            pull.relay(1, 3)
+
+    pull.relay(0, 0)
+    pull.begin(1)
+    for j in range(1, 4):
+        pull.relay(0, j)
+    pull.finish(0)
+    pull.relay(1, 0)
     parts_loop(parts, forward)
+    pull.relay(2, 1)
 
     def middle(at):
         values = ext_ref[pl.ds(at.start + HALO, at.size), :].astype(F32)
@@ -394,27 +722,32 @@
     gffn = out_ref
     gffn_t[...] = gffn[...].T
     two_t[...] = normed_two[...].T
-    normed_t[...] = normed[...].T
+    normed[...] = normed[...].T
+    normed_t = normed
     acc[...] = jnp.zeros_like(acc)
     own_ref[...] = jnp.zeros_like(own_ref)
+    pull.relay(2, 2)
+    pull.relay(2, 3)
+    for p in (1, 2):
+        pull.finish(p)
+    for p in range(3):
+        pull.drain(p)
 
     def feed(m):
-        fetch(wu_hbm, wu, 1, m).wait()
-        fetch(wd_hbm, wd, 2, m).wait()
-        up = jnp.maximum(nn(normed_two[...], wu[m]), 0.0)
+        up = jnp.maximum(nn(normed_two[...], weight(1, m)), 0.0)
         upper[...] = (2.0 * up).astype(BF16)
         hidden[...] = (up * up).astype(BF16)
-        acc[...] += nt(hidden[...], wd[m])
-        gd[m] = nn(gffn_t[...], hidden[...]).astype(BF16)
-        put(gd, gd_hbm, 2, m).start()
-        lower[...] = (nn(gffn[...], wd[m]) * upper[...].astype(F32)).astype(BF16)
-        gu[m] = nn(two_t[...], lower[...]).astype(BF16)
-        put(gu, gu_hbm, 1, m).start()
-        own_ref[...] += nt(lower[...], wu[m])
+        acc[...] += nt(hidden[...], weight(2, m))
+        upper[...] = (nn(gffn[...], weight(2, m)) * upper[...].astype(F32)).astype(BF16)
+        store(2, m, slice(0, width), nn(gffn_t[...], hidden[...]).astype(BF16))
+        own_ref[...] += nt(upper[...], weight(1, m))
+        store(1, m, slice(0, width), nn(two_t[...], upper[...]).astype(BF16))
 
     parts_loop(parts, feed)
-
-    gain_ref[...] = jnp.zeros_like(gain_ref)
+    push.start(2)
+    push.start(1)
+
+    small_ref[...] = jnp.zeros_like(small_ref)
 
     def turn(at):
         value = resid[at, :]
@@ -422,9 +755,9 @@
         scale = rms(value)
         hat = value * scale
         grad = own_ref[at, :]
-        gain_ref[0:1, :] += jnp.sum(grad * hat, axis=0, keepdims=True)
+        small_ref[0, 4:5, :] += jnp.sum(grad * hat, axis=0, keepdims=True)
         total = grad_ref[at, :].astype(F32) + rms_back(grad, gain_two, hat, scale)
-        resid_grad_ref[at, :] = total
+        tokens_out[at, :] = total
         out_ref[at, :] = (value + filled * acc[at, :]).astype(BF16)
         normed_two[at, :] = (filled * total).astype(BF16)
 
@@ -435,7 +768,24 @@
     acc[...] = jnp.zeros_like(acc)
 
     def backward(m):
-        grads = nn(gattn[...], wa[m, :, : 2 * BLK]).astype(BF16)
+        @pl.when(m == 0)
+        def _():
+            push.met(2)
+            for k in ks:
+                push.step_one(2, k)
+
+        @pl.when(m == 1)
+        def _():
+            push.met(1)
+            for k in ks:
+                push.step_one(1, k)
+
+        @pl.when(m == 3)
+        def _():
+            for k in ks:
+                push.step_two(2, k)
+
+        grads = nn(gattn[...], lanes_of(0, m, slice(0, 2 * BLK))).astype(BF16)
         hidden[:, : 2 * BLK] = grads
         wide[...] = jnp.zeros_like(wide)
         for at in range(tiles):
@@ -459,76 +809,131 @@
             one = grad * cols_ref[:, 0:1]
             two = grad * cols_ref[:, 1:2]
             source = proj[m, :, blk(c)].astype(F32)
-            small_ref[m, 0:1, blk(c)] = jnp.sum(grad * source, axis=0, keepdims=True)
-            small_ref[m, 1:2, blk(c)] = jnp.sum(one * pltpu.roll(source, 1, 0), axis=0, keepdims=True)
-            small_ref[m, 2:3, blk(c)] = jnp.sum(two * pltpu.roll(source, 2, 0), axis=0, keepdims=True)
+            small_ref[m, 0:1, blk(c + 1)] = jnp.sum(grad * source, axis=0, keepdims=True)
+            small_ref[m, 1:2, blk(c + 1)] = jnp.sum(one * pltpu.roll(source, 1, 0), axis=0, keepdims=True)
+            small_ref[m, 2:3, blk(c + 1)] = jnp.sum(two * pltpu.roll(source, 2, 0), axis=0, keepdims=True)
             mixed[m, :, blk(c)] = (
                 kernel_ref[m, 0:1, blk(c)] * grad
                 + kernel_ref[m, 1:2, blk(c)] * pltpu.roll(one, span - 1, 0)
                 + kernel_ref[m, 2:3, blk(c)] * pltpu.roll(two, span - 2, 0)
             ).astype(BF16)
+        own_ref[...] += nt(mixed[m, HALO:, :], lanes_of(0, m, slice(BLK, width)))
+        acc[:HALO, :] += nt(mixed[m, :HALO, :], lanes_of(0, m, slice(BLK, width)))
         part = nn(two_t[...], heads[m])
-        whole = nn(normed_t[...], mixed[m])
-        ga[m, :, blk(0)] = part[:, blk(0)].astype(BF16)
-        ga[m, :, blk(1)] = (half_of(part[:, blk(1)], False) + half_of(whole[:, blk(0)], True)).astype(BF16)
-        ga[m, :, 2 * BLK :] = whole[:, BLK:].astype(BF16)
-        put(ga, ga_hbm, 0, m).start()
-        own_ref[...] += nt(mixed[m, HALO:, :], wa[m, :, BLK:])
-        acc[:HALO, :] += nt(mixed[m, :HALO, :], wa[m, :, BLK:])
+        wide[...] = nn(normed_t[...], mixed[m])
+        store(0, m, blk(0), part[:, blk(0)].astype(BF16))
+        store(0, m, blk(1), (half_of(part[:, blk(1)], False) + half_of(wide[:, blk(0)], True)).astype(BF16))
+        store(0, m, slice(2 * BLK, width), wide[:, BLK:].astype(BF16))
 
     parts_loop(parts, backward)
-    pass_ref[...] = acc[:HALO, :].astype(BF16)
-    for m in range(parts):
-        put(ga, ga_hbm, 0, m).wait()
-        put(gu, gu_hbm, 1, m).wait()
-        put(gd, gd_hbm, 2, m).wait()
-
-
-def layer_call(wa, wu, wd, ext, grad_out, cols, seg_row, gains, kernel):
-    parts, width, _ = wa.shape
-    rows = grad_out.shape[0]
+    push.start(0)
+    sent[...] = acc[:HALO, :].astype(BF16)
+
+    def gain_rows(at, grad):
+        values = ext_ref[at, :].astype(F32)
+        small_ref[0, 3:4, :] += jnp.sum(grad * (values * rms(values)), axis=0, keepdims=True)
+
+    rows_loop(HALO, 128, lambda at: gain_rows(at, acc[at, :]))
+    rows_loop(rows, 128, lambda at: gain_rows(pl.ds(at.start + HALO, at.size), own_ref[at, :]))
+    for m in range(1, parts):
+        small_ref[m, 3:5, :] = small_ref[0, 3:5, :]
+    back_on = neighbour(sent, passed, 2, parts - 1)
+    back_on.start()
+    small.begin()
+    push.met(0)
+    for k in ks:
+        push.step_one(0, k)
+        push.step_two(1, k)
+    small.middle()
+
+    def last(at, extra):
+        values = tok_ref[at, :].astype(F32)
+        scale = rms(values)
+        tokens_out[at, :] += rms_back(own_ref[at, :] + extra, gain_one, values * scale, scale)
+
+    def end_rows(at):
+        keep = jnp.where(me < parts - 1, 1.0, 0.0)
+        last(pl.ds(at.start + rows - HALO, at.size), passed[at, :].astype(F32) * keep)
+
+    rows_loop(rows - HALO, 128, lambda at: last(at, 0.0))
+    small.later()
+    for k in ks:
+        push.step_three(2, k)
+        push.step_two(0, k)
+        push.step_three(1, k)
+    back_on.wait()
+    rows_loop(HALO, 128, end_rows)
+    push.step_four(2, own_out)
+    for k in ks:
+        push.step_three(0, k)
+    push.step_four(1, own_out)
+    small.finish(small_out)
+    push.step_four(0, own_out)
+    for p in range(3):
+        push.drain(p)
+
+
+def layer_call(pieces, tokens, grad_out, cols, seg_row, gains, kernel):
+    parts = lax.axis_size("mp")
+    rows, width = grad_out.shape
     span = rows + HALO
     tiles = rows // SEQ_MAX
+    zs = lax.axis_size("batch") // 2
+    copies = 8 * zs - 1
+    shard = width // (2 * zs)
+    half = shard // 2
     vmem = pl.BlockSpec(memory_space=pltpu.VMEM)
-    hbm = pl.BlockSpec(memory_space=pl.ANY)
-    big = pltpu.VMEM((parts, width, width), BF16)
     return pl.pallas_call(
         layer_kernel,
-        in_specs=[hbm] * 3 + [vmem] * 6,
-        out_specs=[hbm] * 3 + [vmem] * 6,
-        out_shape=[jax.ShapeDtypeStruct((parts, width, width), BF16)] * 3
-        + [
+        in_specs=[vmem] * 7,
+        out_specs=[vmem] * 4,
+        out_shape=[
             jax.ShapeDtypeStruct((rows, width), BF16),
             jax.ShapeDtypeStruct((rows, width), F32),
-            jax.ShapeDtypeStruct((rows, width), F32),
-            jax.ShapeDtypeStruct((HALO, width), BF16),
-            jax.ShapeDtypeStruct((parts, 3, COLUMNS), F32),
-            jax.ShapeDtypeStruct((1, width), F32),
+            jax.ShapeDtypeStruct((3, shard, width), F32),
+            jax.ShapeDtypeStruct((8, width), F32),
         ],
         scratch_shapes=[
-            big, big, big, big, big, big,
+            pltpu.VMEM((3, 2, 2, zs, 2, shard, width), BF16),
+            pltpu.VMEM((span, width), BF16),
             pltpu.VMEM((span, width), BF16),
             pltpu.VMEM((parts, span, COLUMNS), BF16),
             pltpu.VMEM((parts, span, COLUMNS), BF16),
             pltpu.VMEM((parts, tiles, 3, 2 * SEQ_MAX, SEQ_MAX), BF16),
             pltpu.VMEM((parts, rows, 2 * BLK), BF16),
-            pltpu.VMEM((tiles, 2 * SEQ_MAX, SEQ_MAX), F32),
+            pltpu.VMEM((tiles, 2 * SEQ_MAX, SEQ_MAX), BF16),
             pltpu.VMEM((span, COLUMNS), F32),
             pltpu.VMEM((rows, width), F32),
             pltpu.VMEM((rows, width), F32),
             pltpu.VMEM((rows, width), BF16),
             pltpu.VMEM((width, rows), BF16),
             pltpu.VMEM((width, rows), BF16),
-            pltpu.VMEM((width, span), BF16),
             pltpu.VMEM((rows, width), BF16),
             pltpu.VMEM((rows, width), BF16),
-            pltpu.VMEM((rows, width), BF16),
-            pltpu.SemaphoreType.DMA((3, parts)),
-            pltpu.SemaphoreType.DMA((3, parts)),
+            pltpu.VMEM((3, 2, zs, 2, shard, width), BF16),
+            pltpu.VMEM((3, zs, 2, 2, half, width), BF16),
+            pltpu.VMEM((3, zs, 2, half, width), BF16),
+            pltpu.VMEM((3, zs - 1, 2, half, width), BF16),
+            pltpu.VMEM((HALO, width), BF16),
+            pltpu.VMEM((HALO, width), BF16),
+            pltpu.VMEM((parts, 8, width), F32),
+            pltpu.VMEM((2, 8, width), F32),
+            pltpu.VMEM((2, 8, width), F32),
+            pltpu.VMEM((8, width), F32),
+            pltpu.VMEM((2 * zs - 1, 8, width), F32),
+            pltpu.SemaphoreType.DMA((3, 2, copies)),
+            pltpu.SemaphoreType.DMA((3, 2, copies)),
+            pltpu.SemaphoreType.DMA((3,)),
+            pltpu.SemaphoreType.DMA((4,)),
+            pltpu.SemaphoreType.DMA((2, 3, 2)),
+            pltpu.SemaphoreType.DMA((2, 3, zs, 6)),
+            pltpu.SemaphoreType.DMA((2, 2 + 2 * zs)),
         ],
-        compiler_params=pltpu.CompilerParams(vmem_limit_bytes=67043328),
+        compiler_params=pltpu.CompilerParams(
+            vmem_limit_bytes=67043328, collective_id=0, has_side_effects=True
+        ),
         name="layer",
-    )(wa, wu, wd, ext, grad_out, cols, seg_row, gains, kernel)
+    )(pieces, tokens, grad_out, cols, seg_row, gains, kernel)
 
 
 def arrange(q, k, v, o):
@@ -554,7 +959,8 @@
     shard = w_qkv.shape[0]
     fits = (
         rows % SEQ_MAX == 0 and part == 3 * HD and width == 4 * part and shard % 16 == 0
-        and w_up.shape[1] == width and seg_ids.shape[0] == n_mp * rows
+        and w_up.shape[1] == width and seg_ids.shape[0] == n_mp * rows and shard % 32 == 0 and n_batch % 2 == 0
+        and rows + HALO == width
     )
     if not fits:
         return shards_plain(
@@ -563,12 +969,9 @@
     own_start = lax.axis_index("mp") * rows
     piece_a = arrange(w_qkv[:, 0], w_qkv[:, 1], w_qkv[:, 2], w_out.T)
     pieces = jnp.stack([piece_a, w_up, w_down.T])
-    wa, wu, wd = gather(pieces)
     taps = lax.all_gather(dconv_kernel, "mp", axis=0, tiled=False)
     zero = jnp.zeros_like(taps[:, 0])
     kernel = arrange(taps[:, 0], taps[:, 1], taps[:, 2], zero)[..., BLK:]
-    back = [(i, i + 1) for i in range(n_mp - 1)]
-    ext = jnp.concatenate([lax.ppermute(tokens[rows - HALO :], "mp", back), tokens], axis=0)
     seg_pad = jnp.concatenate([jnp.full((HALO,), -1, jnp.int32), seg_ids])
     seg = lax.dynamic_slice_in_dim(seg_pad, own_start, HALO + rows, 0).astype(F32)
     slot = own_start - HALO + lax.iota(jnp.int32, HALO + rows)
@@ -582,52 +985,24 @@
         axis=1,
     )
     gains = jnp.stack([gain_attn, gain_ffn])
-    ga, gu, gd, layer_out, resid_grad, own_normed, passed, taps_grad, gain_two = layer_call(
-        wa, wu, wd, ext, grad_out, cols, seg[None, HALO:], gains, kernel
-    )
-    own = scatter(ga, gu, gd)
-    ahead = [(i + 1, i) for i in range(n_mp - 1)]
-    passed = lax.ppermute(passed, "mp", ahead).astype(F32)
-    own_normed = own_normed + jnp.pad(passed, ((rows - HALO, 0), (0, 0)))
-    values = tokens.astype(F32)
-    scale = rms(values)
-    hat = values * scale
-    grad_tokens = resid_grad + rms_back(own_normed, gain_attn, hat, scale)
-    gain_one = jnp.sum(own_normed * hat, axis=0)
-    first, second, third, _ = disarrange(jnp.pad(taps_grad, ((0, 0), (0, 0), (BLK, 0))))
-    small = jnp.stack([first, second, third]).transpose(0, 2, 1, 3).reshape(9, width)
-    small = jnp.concatenate([small, gain_one[None], gain_two])
-    piece = width // (n_mp * n_batch)
-    small = small.reshape(11, n_mp * n_batch, piece).transpose(1, 0, 2)
-    small = lax.psum_scatter(small, ("mp", "batch"), scatter_dimension=0, tiled=False)
+    layer_out, grad_tokens, own, small = layer_call(pieces, tokens, grad_out, cols, seg[None, HALO:], gains, kernel)
+    first, second, third, _ = disarrange(small[:3])
+    piece = part // n_batch
+    at_piece = lax.axis_index("batch") * piece
+    taps_grad = lax.dynamic_slice_in_dim(jnp.stack([first, second, third]), at_piece, piece, 2)
+    gain_grads = lax.dynamic_slice_in_dim(small[3:5], lax.axis_index("mp") * part + at_piece, piece, 1)
     q, k, v, o = disarrange(own[0])
     return (
         layer_out,
         grad_tokens,
-        small[9],
-        small[10],
+        gain_grads[0],
+        gain_grads[1],
         jnp.stack([q, k, v], axis=1),
-        small[:9].reshape(3, 3, piece),
+        taps_grad,
         o.T,
         own[1],
         own[2].T,
     )
-
-
-def gather(pieces):
-    full = lax.all_gather(pieces, ("batch", "mp"), axis=0, tiled=False)
-    n_mp = lax.axis_size("mp")
-    full = full.reshape((-1, n_mp) + pieces.shape).transpose(2, 1, 0, 3, 4)
-    full = full.reshape(3, n_mp, -1, pieces.shape[2])
-    return full[0], full[1], full[2]
-
-
-def scatter(ga, gu, gd):
-    n_mp, width, columns = ga.shape
-    n_batch = lax.axis_size("batch")
-    grads = jnp.stack([ga, gu, gd]).reshape(3, n_mp, n_batch, width // n_batch, columns)
-    grads = grads.transpose(2, 1, 0, 3, 4).reshape((-1, 3, width // n_batch, columns))
-    return lax.psum_scatter(grads, ("batch", "mp"), scatter_dimension=0, tiled=False).astype(F32)
 
 
 def solution(mesh):

time: 377 us -> 224 us (0.59)
  waiting for transfers between devices: 199 us -> 0 us
  Pallas kernels: 63.2 us -> 201 us
  blocking collectives: 52.7 us -> 6.19 us
  local copies, waits for them, and re-layouts: 26.7 us -> 10.8 us
  between operations: 15.1 us -> 1.55 us
  other arithmetic: 16.2 us -> 4.02 us
  starting transfers between devices: 3.79 us -> 0 us
    pallas_call x1, Pallas kernels: 63.2 us -> 201 us  [layer_call(): pl.pallas_call(layer_kernel, in_specs=[vmem] * 7, out_specs=[vmem] * 4, o...]
    reduce_scatter x1 -> x0, waiting for transfers between devices: 105 us -> none  [scatter(): lax.psum_scatter(grads, ('batch', 'mp'), scatter_dimension=0, tiled=False)]
    all_gather x1 -> x0, waiting for transfers between devices: 91.5 us -> none  [gather(): full = lax.all_gather(pieces, ('batch', 'mp'), axis=0, tiled=False)]
    unnamed x1 -> x0, blocking collectives: 46.2 us -> none
    reshape x2 -> x0, local copies, waits for them, and re-layouts: 7.36 us -> none  [the longest x1 6.76 us: gather(): full = full.reshape((-1, n_mp) + pieces.shape).transpose(2, 1, 0, 3, 4)]
    transpose x3 -> x0, other arithmetic: 6.73 us -> none  [the longest x1 6.7 us: scatter(): grads.transpose(2, 1, 0, 3, 4).reshape((-1, 3, width // n_batch, columns))]
    transpose x3 -> x1, local copies, waits for them, and re-layouts: 5.65 us -> 0.01 us  [shards(): return (layer_out, grad_tokens, gain_grads[0], gain_grads[1], jnp.stack([...]
    slice x3 -> x1, local copies, waits for them, and re-layouts: 5.53 us -> 0.74 us  [shards(): small[3:5]]
  transfers between devices with their start and end apart: 4 -> 0, of which waited for: 3 -> 0; matrix products, arithmetic and copies ran while one was open for 3% -> 0% of each run, Pallas kernels for 0% -> 0%
where the time goes in v4:
time: 224 us; the launch traced here: 223 us
  Pallas kernels  201 us (90%)
  local copies, waits for them, and re-layouts  10.8 us (5%)
  blocking collectives  6.19 us (3%)
  other arithmetic  4.02 us (2%)
    pallas_call x1, Pallas kernels, layer_call(): pl.pallas_call(layer_kernel, in_specs=[vmem] * 7, out_specs=[vmem] * 4, o...  201 us
    all_gather x1, blocking collectives, shards(): taps = lax.all_gather(dconv_kernel, 'mp', axis=0, tiled=False)  6.19 us

profile of v4, /device:TPU:0, one launch (start us, length us, event | category | flops | bytes accessed | tf_op | source)
XLA Modules:
  0.0 223.3 jit_solution(11463082939175152020)
XLA Ops:
  0.6 0.0 copy-start.2
  0.7 0.0 copy-start.5
  0.7 0.0 copy-start.6
  0.7 0.0 copy-start.4
  0.7 0.9 copy.30
  1.6 0.9 slice_bitcast_fusion.5
  2.5 0.1 concatenate.42
  2.6 1.8 pad_maximum_fusion.pieces_ref
  5.1 0.0 copy-done.2
  5.1 0.1 fusion.2
  5.2 0.1 fusion.4
  5.3 0.2 scatter.9
  5.5 0.9 copy.34.cols_ref
  6.5 0.6 slice.183
  7.1 0.0 copy-done.5
  7.1 0.0 copy-done.6
  7.1 0.6 pad_maximum_fusion.3.gains_ref
  7.7 0.0 copy-done.4
  7.7 6.2 %all-gather = f32[12,3,192]{2,1,0:T(4,128)S(1)} all-gather(f32[3,3,192]{2,1,0:T(4,128)S(1)} %copy-done.4), channel_id=2, replica_groups=mesh['mp'=4,'batch'=8] {'mp'}, dimensions={0}, use_global_device_ids=true | all-gather | bytes 34560 | tf_op jit(solution)/shard_map/all_gather | solution.py:972
  14.0 0.7 concatenate.46.kernel_ref
  14.7 200.7 %layer.1 = (bf16[512,768]{1,0:T(8,128)(2,1)}, f32[512,768]{1,0:T(8,128)}, f32[3,96,768]{2,1,0:T(8,128)}, f32[8,768]{1,0:T(8,128)}) custom-call(bf16[3,96,768]{2,1,0:T(8,128)(2,1)} %pad_maximum_fusion.pieces_ref, bf16[512,768]{1,0:T(8,128)(2,1)} %tok_ref.1, bf16[512,768]{1,0:T(8,128)(2,1)} %grad_ref.1, f32[768,4]{1,0:T(8,128)} %copy.34.cols_ref, ...), custom_call_target="tpu_custom_call" | custom-call | tf_op jit(solution)/shard_map/layer/pallas_call | solution.py:886
  215.4 0.7 slice.192
  216.1 0.1 constant_dynamic-slice_fusion
  216.2 0.5 slice_bitcast_fusion.12
  216.7 0.0 copy-start.3
  216.7 0.0 copy-start.1
  216.7 2.1 slice_bitcast_fusion
  218.8 0.0 copy-start
  218.8 0.1 fusion.6
  219.0 0.7 pad_maximum_fusion.1
  219.7 0.0 copy-done.3
  219.7 0.1 fusion.8
  219.8 0.7 fusion.1
  220.5 0.7 copy.35
  221.2 0.0 copy-done.1
  221.2 0.9 copy.44
  222.1 0.0 copy-done
  222.1 1.1 copy.45
  (25 shorter events, 0.2 us)
Async XLA Ops:
  0.6 4.4 %copy-start.2 = (s32[2048]{0:T(1024)S(1)}, s32[2048]{0:T(1024)}, u32[]{:S(2)}) copy-start(s32[2048]{0:T(1024)} %param.16) | copy-start | bytes 24580
  0.7 6.4 %copy-start.5 = (f32[768]{0:T(1024)S(1)}, f32[768]{0:T(1024)}, u32[]{:S(2)}) copy-start(f32[768]{0:T(1024)} %param.19) | copy-start | bytes 9220
  0.7 6.4 %copy-start.6 = (f32[768]{0:T(1024)S(1)}, f32[768]{0:T(1024)}, u32[]{:S(2)}) copy-start(f32[768]{0:T(1024)} %param.18) | copy-start | bytes 9220
  0.7 7.0 %copy-start.4 = (f32[3,3,192]{2,1,0:T(4,128)S(1)}, f32[3,3,192]{2,1,0:T(4,128)}, u32[]{:S(2)}) copy-start(f32[3,3,192]{2,1,0:T(4,128)} %param.21) | copy-start | bytes 20740
  216.7 3.0 %copy-start.3 = (f32[8,768]{1,0:T(8,128)S(1)}, f32[8,768]{1,0:T(8,128)}, u32[]{:S(2)}) copy-start(f32[8,768]{1,0:T(8,128)} %get-tuple-element.39) | copy-start | bytes 73732
  216.7 4.5 %copy-start.1 = (bf16[512,768]{1,0:T(8,128)(2,1)S(1)}, bf16[512,768]{1,0:T(8,128)(2,1)}, u32[]{:S(2)}) copy-start(bf16[512,768]{1,0:T(8,128)(2,1)} %get-tuple-element.104) | copy-start | bytes 2359300
  218.8 3.3 %copy-start = (f32[512,768]{1,0:T(8,128)S(1)}, f32[512,768]{1,0:T(8,128)}, u32[]{:S(2)}) copy-start(f32[512,768]{1,0:T(8,128)} %get-tuple-element.105) | copy-start | bytes 4718596

commit v5 on v4

--- a/solution.py
+++ b/solution.py
@@ -602,12 +602,12 @@
 
 
 def layer_kernel(
-    pieces_ref, tok_ref, grad_ref, cols_ref, seg_row_ref, gains_ref, kernel_ref,
+    pieces_ref, tok_ref, grad_ref, cols_ref, seg_row_ref, gains_ref, taps_ref,
     out_ref, tokens_out, own_out, small_out,
     w, ext_ref, normed, proj, mixed, prob, heads, bias, wide, acc, own_ref, normed_two,
     gffn_t, two_t, hidden, upper, one, two, three, four, sent, passed,
-    small_ref, s_sums, s_one, s_two, s_three,
-    send_sems, recv_sems, own_sems, halo_sems, one_sems, sems, small_sems,
+    small_ref, s_sums, s_one, s_two, s_three, kernel_ref,
+    send_sems, recv_sems, own_sems, halo_sems, one_sems, sems, small_sems, taps_sems,
 ):
     parts = w.shape[1] * w.shape[2]
     rows, width = tokens_out.shape
@@ -638,7 +638,16 @@
             device_id={"mp": lax.rem(me + by, parts)}, device_id_type=MESH,
         )
 
+    def taps_copy(by):
+        return pltpu.make_async_remote_copy(
+            taps_ref, kernel_ref.at[me], taps_sems.at[0, by - 1], taps_sems.at[1, by - 1],
+            device_id={"mp": lax.rem(me + by, parts)}, device_id_type=MESH,
+        )
+
     meet_all()
+    for by in range(1, parts):
+        taps_copy(by).start()
+    kernel_ref[me] = taps_ref[...]
     pull.begin_z(0)
     pull.begin(0)
     pass_on = neighbour(tok_ref.at[rows - HALO :], ext_ref.at[:HALO], 0, 1)
@@ -655,6 +664,10 @@
         normed[at, :] = (values * rms(values) * gain_one).astype(BF16)
 
     pass_on.wait()
+    for by in range(1, parts):
+        other = kernel_ref.at[lax.rem(me + parts - by, parts)]
+        pltpu.make_async_copy(other, other, taps_sems.at[1, by - 1]).wait()
+        taps_copy(by).wait_send()
     rows_loop(span, 128, norm_one)
     for at in range(tiles):
         key = lax.broadcasted_iota(jnp.int32, (2 * tile, tile), 0)
@@ -777,13 +790,14 @@
         @pl.when(m == 1)
         def _():
             push.met(1)
-            for k in ks:
-                push.step_one(1, k)
-
-        @pl.when(m == 3)
+            push.step_one(1, ks[0])
+
+        @pl.when(m == 2)
         def _():
             for k in ks:
                 push.step_two(2, k)
+            for k in ks[1:]:
+                push.step_one(1, k)
 
         grads = nn(gattn[...], lanes_of(0, m, slice(0, 2 * BLK))).astype(BF16)
         hidden[:, : 2 * BLK] = grads
@@ -840,10 +854,12 @@
     back_on = neighbour(sent, passed, 2, parts - 1)
     back_on.start()
     small.begin()
+    for k in ks:
+        push.step_three(2, k)
     push.met(0)
     for k in ks:
+        push.step_two(1, k)
         push.step_one(0, k)
-        push.step_two(1, k)
     small.middle()
 
     def last(at, extra):
@@ -857,17 +873,17 @@
 
     rows_loop(rows - HALO, 128, lambda at: last(at, 0.0))
     small.later()
-    for k in ks:
-        push.step_three(2, k)
-        push.step_two(0, k)
-        push.step_three(1, k)
     back_on.wait()
     rows_loop(HALO, 128, end_rows)
+    for k in ks:
+        push.step_three(1, k)
     push.step_four(2, own_out)
+    for k in ks:
+        push.step_two(0, k)
+    small.finish(small_out)
     for k in ks:
         push.step_three(0, k)
     push.step_four(1, own_out)
-    small.finish(small_out)
     push.step_four(0, own_out)
     for p in range(3):
         push.drain(p)
@@ -921,6 +937,7 @@
             pltpu.VMEM((2, 8, width), F32),
             pltpu.VMEM((8, width), F32),
             pltpu.VMEM((2 * zs - 1, 8, width), F32),
+            pltpu.VMEM((parts, 8, COLUMNS), F32),
             pltpu.SemaphoreType.DMA((3, 2, copies)),
             pltpu.SemaphoreType.DMA((3, 2, copies)),
             pltpu.SemaphoreType.DMA((3,)),
@@ -928,6 +945,7 @@
             pltpu.SemaphoreType.DMA((2, 3, 2)),
             pltpu.SemaphoreType.DMA((2, 3, zs, 6)),
             pltpu.SemaphoreType.DMA((2, 2 + 2 * zs)),
+            pltpu.SemaphoreType.DMA((2, parts - 1)),
         ],
         compiler_params=pltpu.CompilerParams(
             vmem_limit_bytes=67043328, collective_id=0, has_side_effects=True
@@ -969,9 +987,9 @@
     own_start = lax.axis_index("mp") * rows
     piece_a = arrange(w_qkv[:, 0], w_qkv[:, 1], w_qkv[:, 2], w_out.T)
     pieces = jnp.stack([piece_a, w_up, w_down.T])
-    taps = lax.all_gather(dconv_kernel, "mp", axis=0, tiled=False)
-    zero = jnp.zeros_like(taps[:, 0])
-    kernel = arrange(taps[:, 0], taps[:, 1], taps[:, 2], zero)[..., BLK:]
+    zero = jnp.zeros_like(dconv_kernel[0])
+    kernel = arrange(dconv_kernel[0], dconv_kernel[1], dconv_kernel[2], zero)[:, BLK:]
+    kernel = jnp.pad(kernel, ((0, 5), (0, 0)))
     seg_pad = jnp.concatenate([jnp.full((HALO,), -1, jnp.int32), seg_ids])
     seg = lax.dynamic_slice_in_dim(seg_pad, own_start, HALO + rows, 0).astype(F32)
     slot = own_start - HALO + lax.iota(jnp.int32, HALO + rows)

time: 224 us -> 205 us (0.915)
  Pallas kernels: 201 us -> 187 us
  blocking collectives: 6.19 us -> 0 us
    pallas_call x1, Pallas kernels: 201 us -> 187 us  [layer_call(): pl.pallas_call(layer_kernel, in_specs=[vmem] * 7, out_specs=[vmem] * 4, o...]
    all_gather x1 -> x0, blocking collectives: 6.19 us -> none  [shards(): taps = lax.all_gather(dconv_kernel, 'mp', axis=0, tiled=False)]
where the time goes in v5:
time: 205 us; the launch traced here: 203 us
  Pallas kernels  187 us (91%)
  local copies, waits for them, and re-layouts  10.8 us (5%)
  other arithmetic  4.02 us (2%)
    pallas_call x1, Pallas kernels, layer_call(): pl.pallas_call(layer_kernel, in_specs=[vmem] * 7, out_specs=[vmem] * 4, o...  187 us

profile of v5, /device:TPU:0, one launch (start us, length us, event | category | flops | bytes accessed | tf_op | source)
XLA Modules:
  0.0 203.2 jit_solution(3820083697635253402)
XLA Ops:
  0.6 0.0 copy-start.2
  0.7 0.0 copy-start.5
  0.7 0.0 copy-start.6
  0.7 0.0 copy-start.4
  0.7 0.9 copy.27
  1.6 0.9 slice_bitcast_fusion.5
  2.5 0.1 concatenate.43
  2.6 1.8 pad_maximum_fusion.pieces_ref
  5.1 0.0 copy-done.2
  5.1 0.1 fusion.2
  5.2 0.1 fusion.4
  5.3 0.2 scatter.9
  5.5 0.9 copy.28.cols_ref
  6.5 0.6 slice.183
  7.1 0.0 copy-done.5
  7.1 0.0 copy-done.6
  7.1 0.6 pad_maximum_fusion.3.gains_ref
  7.7 0.0 copy-done.4
  7.7 0.1 concatenate.47
  7.8 0.6 pad.10.taps_ref
  8.4 186.9 %layer.1 = (bf16[512,768]{1,0:T(8,128)(2,1)}, f32[512,768]{1,0:T(8,128)}, f32[3,96,768]{2,1,0:T(8,128)}, f32[8,768]{1,0:T(8,128)}) custom-call(bf16[3,96,768]{2,1,0:T(8,128)(2,1)} %pad_maximum_fusion.pieces_ref, bf16[512,768]{1,0:T(8,128)(2,1)} %tok_ref.1, bf16[512,768]{1,0:T(8,128)(2,1)} %grad_ref.1, f32[768,4]{1,0:T(8,128)} %copy.28.cols_ref, ...), custom_call_target="tpu_custom_call" | custom-call | tf_op jit(solution)/shard_map/layer/pallas_call | solution.py:902
  195.4 0.7 slice.192
  196.1 0.1 constant_dynamic-slice_fusion
  196.2 0.5 slice_bitcast_fusion.12
  196.7 0.0 copy-start.3
  196.7 0.0 copy-start.1
  196.7 2.1 %slice_bitcast_fusion = (f32[768,96]{0,1:T(8,128)}, f32[96,768]{1,0:T(8,128)}, f32[96,768]{1,0:T(8,128)S(1)}) fusion(f32[3,96,768]{2,1,0:T(8,128)} %get-tuple-element.40), kind=kLoop, calls=%fused_computation.2 | loop fusion | bytes 1769472 | tf_op jit(solution)/shard_map/transpose | solution.py:1022
  198.8 0.0 copy-start
  198.8 0.1 fusion.6
  199.0 0.7 pad_maximum_fusion.1
  199.7 0.0 copy-done.3
  199.7 0.1 fusion.8
  199.8 0.7 fusion.1
  200.5 0.7 copy.29
  201.2 0.0 copy-done.1
  201.2 0.9 copy.35
  202.1 0.0 copy-done
  202.1 1.1 copy.36
  (25 shorter events, 0.2 us)
Async XLA Ops:
  0.6 4.4 %copy-start.2 = (s32[2048]{0:T(1024)S(1)}, s32[2048]{0:T(1024)}, u32[]{:S(2)}) copy-start(s32[2048]{0:T(1024)} %param.16) | copy-start | bytes 24580
  0.7 6.4 %copy-start.5 = (f32[768]{0:T(1024)S(1)}, f32[768]{0:T(1024)}, u32[]{:S(2)}) copy-start(f32[768]{0:T(1024)} %param.19) | copy-start | bytes 9220
  0.7 6.4 %copy-start.6 = (f32[768]{0:T(1024)S(1)}, f32[768]{0:T(1024)}, u32[]{:S(2)}) copy-start(f32[768]{0:T(1024)} %param.18) | copy-start | bytes 9220
  0.7 7.0 %copy-start.4 = (f32[3,3,192]{2,1,0:T(4,128)S(1)}, f32[3,3,192]{2,1,0:T(4,128)}, u32[]{:S(2)}) copy-start(f32[3,3,192]{2,1,0:T(4,128)} %param.21) | copy-start | bytes 20740
  196.7 3.0 %copy-start.3 = (f32[8,768]{1,0:T(8,128)S(1)}, f32[8,768]{1,0:T(8,128)}, u32[]{:S(2)}) copy-start(f32[8,768]{1,0:T(8,128)} %get-tuple-element.39) | copy-start | bytes 73732
  196.7 4.5 %copy-start.1 = (bf16[512,768]{1,0:T(8,128)(2,1)S(1)}, bf16[512,768]{1,0:T(8,128)(2,1)}, u32[]{:S(2)}) copy-start(bf16[512,768]{1,0:T(8,128)(2,1)} %get-tuple-element.104) | copy-start | bytes 2359300
  198.8 3.3 %copy-start = (f32[512,768]{1,0:T(8,128)S(1)}, f32[512,768]{1,0:T(8,128)}, u32[]{:S(2)}) copy-start(f32[512,768]{1,0:T(8,128)} %get-tuple-element.105) | copy-start | bytes 4718596
